TPU v7x, 256 devices: a whole 4x4x8 slice. The times are simulated.
256 devices in a mesh: rep: 32 (over x_hi, z, core), tp: 8 (over x_lo, y).
Axes of the slice: x: 4 (x_hi: 2, x_lo: 2; x = x_hi * 2 + x_lo), y: 4, z: 8, core: 2. Of those that a mesh axis runs over, the one named last changes fastest.
Arguments:
- tokens: bfloat16 [32, 1024, 3072], P('rep', 'tp'), may hold values from -100 to 100
- norm_gain: float32 [32, 3072], P('rep'), may hold values from 0.5 to 1.5
- w_query: bfloat16 [32, 3072, 2048], P('rep', None, 'tp'), may hold values from -1 to 1
- key_weight: bfloat16 [32, 3072, 1024], P('rep', None, 'tp'), may hold values from -1 to 1
- value_weight: bfloat16 [32, 3072, 1024], P('rep', None, 'tp'), may hold values from -0.109375 to 0.109375
- attention_gradient: bfloat16 [32, 1024, 2048], P('rep', None, 'tp'), may hold values from -6 to 6
- global_fragment: float32 [512, 3072], P('tp'), may hold values from -6 to 6
- momentum: float32 [512, 3072], P('tp'), may hold values from -3 to 3
- local_fragment: bfloat16 [32, 512, 3072], P('rep', 'tp'), may hold values from -6 to 6
Outputs:
- grad_query_w: bfloat16 [32, 3072, 2048], P('rep', None, 'tp')
- grad_key_w: bfloat16 [32, 3072, 1024], P('rep', None, 'tp')
- grad_value_w: bfloat16 [32, 3072, 1024], P('rep', None, 'tp')
- grad_gain: float32 [32, 3072], P('rep')
- grad_tokens: bfloat16 [32, 1024, 3072], P('rep', 'tp')
- new_global: float32 [512, 3072], P('tp')
- new_momentum: float32 [512, 3072], P('tp')
All inputs are finite; a program needn't handle non-finite values.
Results may differ from a plain program's by a relative error of at most 0.019.
The roundings to bfloat16 on the way count: a program that leaves them out, or rounds other values in their place, can miss the bound.
Values may be sent and summed in bfloat16 or wider, within the bound.
No kernel may reach another device: no remote copies, remote signals or barrier semaphores. Data moves between devices by JAX's collectives and lax.ppermute only.
A program may use at most 128 MiB of HBM per device.

v0:
```python
import functools

import jax
import jax.numpy as jnp
from jax import lax
from jax.experimental import pallas as pl
from jax.experimental.pallas import tpu as pltpu
from jax.sharding import PartitionSpec as P


HEAD_SIZE = 128
A = 1792
MODEL = 3072
B = MODEL - A
SA = 1536
SB = MODEL - SA
SH = 768
SHB = 768
ROWS = 128
SEQ = 1024
TILE = 256
STRIDE = 32
STEP_A = 896
STEP_B = 640

epsilon = 1e-05
rope_base = 500000.0
outer_rate = 0.7
outer_momentum = 0.9


f32 = jnp.float32
bf16 = jnp.bfloat16
NT = (((1,), (1,)), ((), ()))
TN = (((0,), (0,)), ((), ()))
NN = (((1,), (0,)), ((), ()))

BLOCKS = ((0, 0), (1, 0), (0, -1), (0, 1), (1, -1), (1, 1), (0, 2), (1, 2))
WHERE = {block: at for at, block in enumerate(BLOCKS)}


def index(x, y):
    return x * 4 + y % 4


X_PAIRS = [(index(x, y), index(1 - x, y)) for x in range(2) for y in range(4)]
UP_PAIRS = [(index(x, y), index(x, y + 1)) for x in range(2) for y in range(4)]
DOWN_PAIRS = [(index(x, y), index(x, y - 1)) for x in range(2) for y in range(4)]


def across(value):
    return lax.ppermute(value, "tp", X_PAIRS)


def up(value):
    return lax.ppermute(value, "tp", UP_PAIRS)


def down(value):
    return lax.ppermute(value, "tp", DOWN_PAIRS)


def dot(a, b, dims):
    return lax.dot_general(a, b, dims, preferred_element_type=f32)


VMEM_LIMIT = {"attention": 16, "weights": 16, "project_first": 16}
VM = pl.BlockSpec(memory_space=pltpu.VMEM)
SM = pl.BlockSpec(memory_space=pltpu.SMEM)


def call(kernel, name, outs, ins, flops, scratch=(), smem=0):
    nbytes = sum(v.size * v.dtype.itemsize for v in ins) + sum(
        o.size * o.dtype.itemsize for o in outs
    )
    return pl.pallas_call(
        kernel,
        out_shape=tuple(outs),
        in_specs=[SM] * smem + [VM] * (len(ins) - smem),
        out_specs=tuple([VM] * len(outs)),
        scratch_shapes=list(scratch),
        cost_estimate=pl.CostEstimate(flops=flops, bytes_accessed=nbytes, transcendentals=0),
        compiler_params=pltpu.CompilerParams(vmem_limit_bytes=VMEM_LIMIT.get(name, 8) * 1024 * 1024),
    )(*ins)


def shape(*dims, dtype=bf16):
    return jax.ShapeDtypeStruct(dims, dtype)


def each_block(count, body):
    size = 32

    @pl.loop(0, count // size)
    def _(i):
        body(pl.ds(pl.multiple_of(i * size, size), size))


def norm_kernel(tokens, gain, part_a, part_b):
    def body(at):
        wide = tokens[at, :].astype(f32)
        inverse = lax.rsqrt(jnp.mean(wide * wide, axis=-1, keepdims=True) + epsilon)
        part_a[at, :] = (wide[:, :A] * inverse * gain[:, :A]).astype(bf16)
        part_b[at, :] = (wide[:, A:] * inverse * gain[:, A:]).astype(bf16)

    each_block(ROWS, body)


def project_kernel(n, *refs):
    wq, wk, wv, out = refs[-4:]
    rows_a = jnp.concatenate([r[...] for r in refs[:n]], axis=0)
    rows_b = jnp.concatenate([r[...] for r in refs[n:-4]], axis=0)
    out[:, :256] = dot(rows_a, wq[:A, :], NN) + dot(rows_b, wq[A:, :], NN)
    both = jnp.concatenate([wk[...], wv[...]], axis=1)
    out[:, 256:] = dot(rows_a, both[:A, :], NN) + dot(rows_b, both[A:, :], NN)


def join_kernel(low, high, out):
    out[: low.shape[0], :] = low[...]
    out[low.shape[0] :, :] = high[...]


def share_kernel(local, out):
    count = out.shape[1]
    for j in range(out.shape[0]):
        out[j] = local[j * count : (j + 1) * count, :]


def spread_kernel(mine, other, out):
    mean = (mine[...] + other[...]) / (2 * out.shape[0])
    for j in range(out.shape[0]):
        out[j] = mean


def sign_row():
    lane = lax.broadcasted_iota(jnp.int32, (1, HEAD_SIZE), 1)
    return jnp.where(lane < HEAD_SIZE // 2, -1.0, 1.0).astype(f32)


def attention_kernel(
    at, first, second, third, coarse, fine, grad_out, out, qs, ks, vs, dk, dv, cosine, sine
):
    sign = sign_row()
    scale = HEAD_SIZE ** (-0.5)
    fine_cos, fine_sin = fine[:STRIDE, :], fine[STRIDE:, :]
    for a in range(SEQ // STRIDE):
        c, s = coarse[a : a + 1, :], coarse[SEQ // STRIDE + a : SEQ // STRIDE + a + 1, :]
        cosine[a * STRIDE : (a + 1) * STRIDE, :] = c * fine_cos - s * fine_sin
        sine[a * STRIDE : (a + 1) * STRIDE, :] = s * fine_cos + c * fine_sin

    def rotate(v, c, s):
        return v * c + pltpu.roll(v, HEAD_SIZE // 2, 1) * (sign * s)

    def rotate_back(g, c, s):
        return g * c - pltpu.roll(g * s, HEAD_SIZE // 2, 1) * sign

    def place(source, base, j):
        here = pl.ds(pl.multiple_of(at[j] * ROWS, ROWS), ROWS)
        c, s = cosine[here, :], sine[here, :]
        block = source[pl.ds(pl.multiple_of(base, ROWS), ROWS), :]
        qs[here, :128] = rotate(block[:, :128], c, s).astype(bf16)
        qs[here, 128:] = rotate(block[:, 128:256], c, s).astype(bf16)
        ks[here, :] = rotate(block[:, 256:384], c, s).astype(bf16)
        vs[here, :] = block[:, 384:].astype(bf16)

    @pl.loop(0, 4)
    def _(j):
        place(first, j * ROWS, j)

    @pl.loop(0, 2)
    def _(j):
        place(second, j * ROWS, j + 4)
        place(third, j * ROWS, j + 6)

    dk[...] = jnp.zeros_like(dk)
    dv[...] = jnp.zeros_like(dv)
    key_at = lax.broadcasted_iota(jnp.int32, (TILE, TILE), 0)
    query_at = lax.broadcasted_iota(jnp.int32, (TILE, TILE), 1)
    allowed = key_at <= query_at
    for i in range(SEQ // TILE):
        lo, hi = i * TILE, (i + 1) * TILE

        keys, values = ks[:hi, :], vs[:hi, :]
        for h in range(2):
            cols = slice(h * 128, (h + 1) * 128)
            q, g = qs[lo:hi, cols], grad_out[lo:hi, cols]
            scores = dot(keys, q, NT) * scale
            last = jnp.where(allowed, scores[lo:, :], -jnp.inf)
            scores = jnp.concatenate([scores[:lo, :], last], axis=0) if i else last
            powers = jnp.exp(scores - jnp.max(scores, axis=0, keepdims=True))
            probability = powers * (1.0 / jnp.sum(powers, axis=0, keepdims=True))
            dv[:hi, :] += dot(probability.astype(bf16), g, NN)
            grad_prob = dot(values, g, NT)
            row = jnp.sum(grad_prob * probability, axis=0, keepdims=True)
            grad_score = (probability * (grad_prob - row) * scale).astype(bf16)
            dk[:hi, :] += dot(grad_score, q, NN)
            dq = dot(grad_score, keys, TN)
            out[lo:hi, cols] = rotate_back(dq, cosine[lo:hi, :], sine[lo:hi, :]).astype(bf16)

    out[:, 256:384] = rotate_back(dk[...], cosine[...], sine[...]).astype(bf16)
    out[:, 384:] = dv[...].astype(bf16)


def rows_of(at, ref, block):
    return ref[pl.ds(pl.multiple_of(at[WHERE[block]] * ROWS, ROWS), ROWS), :]


def back_tile(rows, wq, wk, wv, cols):
    both = jnp.concatenate([wk[cols, :], wv[cols, :]], axis=1)
    return (dot(rows[:, :256], wq[cols, :], NT) + dot(rows[:, 256:], both, NT)).astype(bf16)


def columns(i, base=0):
    return pl.ds(pl.multiple_of(i * TILE + base, TILE), TILE)


def far_back_kernel(at, grads, wq, wk, wv, far_low, far_high):
    far = jnp.concatenate([rows_of(at, grads, (0, 2)), rows_of(at, grads, (1, 2))], axis=0)

    @pl.loop(0, SH // TILE)
    def _(i):
        far_low[:, columns(i)] = back_tile(far, wq, wk, wv, columns(i))
        far_high[:, columns(i)] = back_tile(far, wq, wk, wv, columns(i, SH))


def other_back_kernel(at, grads, wq, wk, wv, x2, x1m, x0):
    other = jnp.concatenate([rows_of(at, grads, (1, d)) for d in (2, 1, -1, 0)], axis=0)

    @pl.loop(0, SHB // TILE)
    def _(i):
        for base in (0, SHB):
            tile = back_tile(other, wq, wk, wv, columns(i, SA + base))
            x2[:, columns(i, base)] = tile[:ROWS, :]
            x1m[:, columns(i, base)] = tile[ROWS : 3 * ROWS, :]
            x0[:, columns(i, base)] = tile[3 * ROWS :, :]


def near_back_kernel(
    at, grads, wq, wk, wv, up_low, up_high, down_low, down_high, own_a, q2, q1, qm, q0
):
    near = jnp.concatenate(
        [rows_of(at, grads, (x, d)) for d in (1, -1, 0) for x in (0, 1)], axis=0
    )
    mine = jnp.concatenate([rows_of(at, grads, (0, d)) for d in (2, 1, -1, 0)], axis=0)

    @pl.loop(0, SH // TILE)
    def _(i):
        for base, above, below in ((0, up_low, down_low), (SH, up_high, down_high)):
            tile = back_tile(near, wq, wk, wv, columns(i, base))
            above[:, columns(i)] = tile[:256, :]
            below[:, columns(i)] = tile[256:512, :]
            own_a[:, columns(i, base)] = tile[512:, :]

    @pl.loop(0, SHB // TILE)
    def _(i):
        for base in (0, SHB):
            tile = back_tile(mine, wq, wk, wv, columns(i, SA + base))
            for n, ref in enumerate((q2, q1, qm, q0)):
                ref[:, columns(i, base)] = tile[n * ROWS : (n + 1) * ROWS, :]


def weight_kernel(at, *refs):
    parts_a, parts_b = refs[:8], refs[8:15]
    grads, wq, wk, wv, gain, dwq, dwk, dwv, gain_part, ordered = refs[15:]
    for j in range(8):
        ordered[j * ROWS : (j + 1) * ROWS, :] = grads[
            pl.ds(pl.multiple_of(at[j] * ROWS, ROWS), ROWS), :
        ]

    def tile(rows, to, size):
        product = dot(rows, ordered[...], TN)
        where = pl.ds(to, size)
        dwq[where, :] = product[:, :256].astype(bf16)
        dwk[where, :] = product[:, 256:384].astype(bf16)
        dwv[where, :] = product[:, 384:].astype(bf16)
        total = (
            product[:, :128] * wq[where, :128].astype(f32)
            + product[:, 128:256] * wq[where, 128:].astype(f32)
            + product[:, 256:384] * wk[where, :].astype(f32)
            + product[:, 384:] * wv[where, :].astype(f32)
        )
        gain_part[:, where] = jnp.sum(total.T, axis=0, keepdims=True) / gain[:, where]

    @pl.loop(0, A // STEP_A)
    def _(i):
        col = pl.multiple_of(i * STEP_A, 128)
        rows = [r[:, pl.ds(col, STEP_A)] for r in parts_a]
        tile(jnp.concatenate(rows, axis=0), col, STEP_A)

    @pl.loop(0, B // STEP_B)
    def _(i):
        col = pl.multiple_of(i * STEP_B, 128)
        rows = [r[:, pl.ds(col, STEP_B)] for r in parts_b]
        tile(jnp.concatenate(rows, axis=0), pl.multiple_of(A + col, 128), STEP_B)


def near_sum_kernel(up_low, near_low, down_high, near_high, mine, arrived, to_up, to_down):
    count = 2 * ROWS
    to_up[:count, :] = (up_low[...].astype(f32) + near_low[...].astype(f32)).astype(bf16)
    to_down[:count, :] = (down_high[...].astype(f32) + near_high[...].astype(f32)).astype(bf16)
    total = (mine[...].astype(f32) + arrived[...].astype(f32)).astype(bf16)
    to_up[count:, :] = total[:, :SHB]
    to_down[count:, :] = total[:, SHB:]


def b_sum_kernel(q1, qm, r, near_low, near_high, to_up, to_down):
    low, high = slice(0, SHB), slice(SHB, SB)
    size = 32

    @pl.loop(0, ROWS // size)
    def _(i):
        at = pl.ds(pl.multiple_of(i * size, size), size)
        below = pl.ds(pl.multiple_of(i * size + ROWS, size), size)
        near = pl.ds(pl.multiple_of(i * size + 2 * ROWS, size), size)

        def total(q, rows, cols):
            return q[at, cols].astype(f32) + r[rows, cols].astype(f32)

        to_up[at, low] = (total(q1, at, low) + near_low[near, :].astype(f32)).astype(bf16)
        to_up[at, high] = total(q1, at, high).astype(bf16)
        to_down[at, low] = total(qm, below, low).astype(bf16)
        to_down[at, high] = (total(qm, below, high) + near_high[near, :].astype(f32)).astype(bf16)


def a_sum_kernel(own, below_low, above_low, below_high, above_high, mine, other):
    size = 32

    @pl.loop(0, ROWS // size)
    def _(i):
        at = pl.ds(pl.multiple_of(i * size, size), size)
        far = pl.ds(pl.multiple_of(i * size + ROWS, size), size)
        for cols, below, above in (
            (slice(0, SH), below_low, above_low),
            (slice(SH, SA), below_high, above_high),
        ):

            def total(rows):
                return (
                    own[rows, cols].astype(f32)
                    + below[rows, :].astype(f32)
                    + above[rows, :].astype(f32)
                )

            mine[at, cols] = total(at)
            other[at, cols] = total(far).astype(bf16)


def gain_sum_kernel(mine, arrived, out):
    out[...] = mine[...] + arrived[...]


def token_kernel(tokens, gain, own_a, from_x, q0, r0, from_below, from_above, out):
    def body(at):
        wide = tokens[at, :].astype(f32)
        inverse = lax.rsqrt(jnp.mean(wide * wide, axis=-1, keepdims=True) + epsilon)
        hat = wide * inverse
        sum_a = own_a[at, :] + from_x[at, :].astype(f32)
        sum_b = (q0[at, :].astype(f32) + r0[at, :].astype(f32)) + (
            from_below[at, :].astype(f32) + from_above[at, :].astype(f32)
        )
        scaled_a = sum_a * gain[:, :SA]
        scaled_b = sum_b * gain[:, SA:]
        mean = (
            jnp.sum(scaled_a * hat[:, :SA], axis=-1, keepdims=True)
            + jnp.sum(scaled_b * hat[:, SA:], axis=-1, keepdims=True)
        ) / MODEL
        out[at, :SA] = (inverse * (scaled_a - hat[:, :SA] * mean)).astype(bf16)
        out[at, SA:] = (inverse * (scaled_b - hat[:, SA:] * mean)).astype(bf16)

    each_block(ROWS, body)


def outer_kernel(
    mean_parts, fragment, momentum, part, other_part, new_fragment, new_momentum, grad_gain
):
    grad_gain[...] = part[...] + other_part[...]
    count = mean_parts.shape[1]

    @pl.loop(0, mean_parts.shape[0] // 2)
    def _(i):
        rows = pl.ds(pl.multiple_of(i * 2 * count, 2 * count), 2 * count)
        mean = jnp.concatenate([mean_parts[2 * i], mean_parts[2 * i + 1]], axis=0)
        change = outer_momentum * momentum[rows, :] + mean
        new_momentum[rows, :] = change
        new_fragment[rows, :] = fragment[rows, :] - outer_rate * (mean + outer_momentum * change)


def rope_tables(positions, width):
    middle = width // 2
    frequency = rope_base ** (-2.0 * jnp.arange(middle, dtype=f32) / width)
    frequency = jnp.concatenate([frequency, frequency])
    angles = positions.astype(f32)[:, None] * frequency[None, :]
    return jnp.concatenate([jnp.cos(angles), jnp.sin(angles)], axis=0)


def swapped(bit):
    return [(index(x, y), index(x, y ^ bit)) for x in range(2) for y in range(4)]


def body(
    tokens,
    norm_gain,
    w_query,
    key_weight,
    value_weight,
    attention_gradient,
    global_fragment,
    momentum,
    local_fragment,
):
    rows = tokens[0]
    wq, wk, wv = w_query[0], key_weight[0], value_weight[0]
    me = lax.axis_index("tp")
    step_x = jnp.array([b[0] for b in BLOCKS], jnp.int32)
    step_y = jnp.array([b[1] for b in BLOCKS], jnp.int32)
    at = ((me // 4 + step_x) % 2) * 4 + (me % 4 + step_y + 4) % 4

    a00, b00 = call(
        norm_kernel, "norm", [shape(ROWS, A), shape(ROWS, B)], [rows, norm_gain], 10**6
    )
    a10 = across(a00)
    bm = up(b00)
    bp = down(b00)
    am = up(a00)
    ap = down(a00)
    b10 = across(b00)
    half = ROWS // 2
    b2l = up(bm[:half])
    b2h = down(bp[half:])
    (b2,) = call(join_kernel, "join", [shape(ROWS, B)], [b2l, b2h], 10**4)
    (pair,) = call(join_kernel, "pair", [shape(2 * ROWS, B)], [bm, bp], 10**4)
    b1 = across(pair)
    a1m = up(a10)
    a1p = down(a10)
    b12 = across(b2)
    a02 = up(am)
    a12 = down(a1p)

    parts_a = [a00, a10, am, ap, a1m, a1p, a02, a12]
    parts_b = [b00, b10, bm, bp, b1, b2, b12]
    weights = [wq, wk, wv]
    (first,) = call(
        functools.partial(project_kernel, 4),
        "project_first",
        [shape(512, 512, dtype=f32)],
        parts_a[:4] + parts_b[:4] + weights,
        2 * 512 * 512 * MODEL,
    )
    (second,) = call(
        functools.partial(project_kernel, 2),
        "project_second",
        [shape(256, 512, dtype=f32)],
        parts_a[4:6] + [b1] + weights,
        2 * 256 * 512 * MODEL,
    )
    (third,) = call(
        functools.partial(project_kernel, 2),
        "project_third",
        [shape(256, 512, dtype=f32)],
        parts_a[6:] + [b2, b12] + weights,
        2 * 256 * 512 * MODEL,
    )
    coarse = rope_tables(jnp.arange(0, SEQ, STRIDE), HEAD_SIZE)
    fine = rope_tables(jnp.arange(STRIDE), HEAD_SIZE)
    (grads,) = call(
        attention_kernel,
        "attention",
        [shape(SEQ, 512)],
        [at, first, second, third, coarse, fine, attention_gradient[0]],
        10 * SEQ * SEQ * 256,
        scratch=[
            pltpu.VMEM((SEQ, 256), bf16),
            pltpu.VMEM((SEQ, 128), bf16),
            pltpu.VMEM((SEQ, 128), bf16),
        ]
        + [pltpu.VMEM((SEQ, 128), f32)] * 4,
        smem=1,
    )
    far_low, far_high = call(
        far_back_kernel,
        "back_far",
        [shape(256, SH), shape(256, SA - SH)],
        [at, grads] + weights,
        2 * 512 * 256 * SA,
        smem=1,
    )
    x2, x1m, x0 = call(
        other_back_kernel,
        "back_other",
        [shape(ROWS, SB), shape(2 * ROWS, SB), shape(ROWS, SB)],
        [at, grads] + weights,
        2 * 512 * 512 * SB,
        smem=1,
    )
    near_low = up(far_low)
    near_high = down(far_high)
    r2 = across(x2)
    r1m = across(x1m)
    r0 = across(x0)
    up_low, up_high, down_low, down_high, own_a, q2, q1, qm, q0 = call(
        near_back_kernel,
        "back_near",
        [shape(256, SH), shape(256, SA - SH)] * 2 + [shape(256, SA)] + [shape(ROWS, SB)] * 4,
        [at, grads] + weights,
        2 * 512 * (768 * SA + 512 * SB),
        smem=1,
    )
    below_high = up(up_high)
    above_low = down(down_low)
    to_up, to_down = call(
        near_sum_kernel,
        "near_sum",
        [shape(3 * ROWS, SH)] * 2,
        [up_low, near_low, down_high, near_high, q2, r2],
        10**5,
    )
    below_low = up(to_up)
    above_high = down(to_down)
    b_up, b_down = call(
        b_sum_kernel,
        "b_sum",
        [shape(ROWS, SB)] * 2,
        [q1, qm, r1m, below_low, above_high],
        10**5,
    )
    from_below = up(b_up)
    from_above = down(b_down)
    own_sum, other_sum_a = call(
        a_sum_kernel,
        "a_sum",
        [shape(ROWS, SA, dtype=f32), shape(ROWS, SA)],
        [own_a, below_low, above_low, below_high, above_high],
        10**5,
    )
    from_x = across(other_sum_a)

    grad_wq, grad_wk, grad_wv, gain_part = call(
        weight_kernel,
        "weights",
        [shape(MODEL, 256), shape(MODEL, 128), shape(MODEL, 128), shape(1, MODEL, dtype=f32)],
        [at] + parts_a + parts_b + [grads] + weights + [norm_gain],
        2 * SEQ * 512 * MODEL,
        scratch=[pltpu.VMEM((SEQ, 512), bf16)],
        smem=1,
    )
    gain_row = [shape(1, MODEL, dtype=f32)]
    arrived_gain = lax.ppermute(gain_part, "tp", X_PAIRS)
    (gain_part,) = call(gain_sum_kernel, "e_sum0", gain_row, [gain_part, arrived_gain], 10**4)
    arrived_gain = lax.ppermute(gain_part, "tp", swapped(1))
    (gain_part,) = call(gain_sum_kernel, "e_sum1", gain_row, [gain_part, arrived_gain], 10**4)
    arrived_gain = lax.ppermute(gain_part, "tp", swapped(2))
    (grad_rows,) = call(
        token_kernel,
        "tokens",
        [shape(ROWS, MODEL)],
        [rows, norm_gain, own_sum, from_x, q0, r0, from_below, from_above],
        10**6,
    )

    replicas = lax.axis_size("rep")
    near = replicas // 2
    groups = [list(range(near)), list(range(near, replicas))]
    count = global_fragment.shape[0] // near
    (parts,) = call(
        share_kernel, "share", [shape(near, count, MODEL)], [local_fragment[0]], 10**4
    )
    arrived = lax.all_to_all(
        parts, "rep", split_axis=0, concat_axis=0, tiled=True, axis_index_groups=groups
    )
    offset = lax.axis_index("rep") % near * count
    global_rows = lax.dynamic_slice_in_dim(global_fragment, offset, count, 0)
    half_sum = jnp.sum(global_rows[None] - arrived.astype(f32), axis=0)
    other_sum = lax.ppermute(half_sum, "rep", [(i, (i + near) % replicas) for i in range(replicas)])
    (copies,) = call(
        spread_kernel, "spread", [shape(near, count, MODEL, dtype=f32)], [half_sum, other_sum], 10**4
    )
    mean = lax.all_to_all(
        copies, "rep", split_axis=0, concat_axis=0, tiled=True, axis_index_groups=groups
    )
    new_global, new_momentum, grad_gain = call(
        outer_kernel,
        "outer",
        [shape(*momentum.shape, dtype=f32)] * 2 + gain_row,
        [mean, global_fragment, momentum, gain_part, arrived_gain],
        10**5,
    )
    return (
        grad_wq[None],
        grad_wk[None],
        grad_wv[None],
        grad_gain,
        grad_rows[None],
        new_global,
        new_momentum,
    )


def solution(mesh):
    placed = (
        P("rep", "tp", None),
        P("rep", None),
        P("rep", None, "tp"),
        P("rep", None, "tp"),
        P("rep", None, "tp"),
        P("rep", None, "tp"),
        P("tp", None),
        P("tp", None),
        P("rep", "tp", None),
    )

    return jax.shard_map(
        body,
        mesh=mesh,
        in_specs=placed,
        out_specs=(
            P("rep", None, "tp"),
            P("rep", None, "tp"),
            P("rep", None, "tp"),
            P("rep", None),
            P("rep", "tp", None),
            P("tp", None),
            P("tp", None),
        ),
        check_vma=False,
    )
```

profile of v0, /device:TPU:24, one launch (start us, length us, event | category | flops | bytes accessed | tf_op | source)
XLA Modules:
  0.0 163.1 jit_solution(9830256469157870463)
XLA Ops:
  0.6 1.1 copy-done.3
  1.8 0.7 copy-done.15
  2.5 1.5 shard_map.162
  3.9 0.7 collective-permute-start.9
  4.7 2.5 %collective-permute-start.8 = (bf16[128,1280]{1,0:T(8,128)(2,1)}, bf16[128,1280]{1,0:T(8,128)(2,1)}, u32[]{:S(2)}, u32[]{:S(2)}) collective-permute-start(bf16[128,1280]{1,0:T(8,128)(2,1)} %get-tuple-element.37.refs_4_.refs_8_), channel_id=1, source_target_pairs={{0,1},{1,2},{2,3},{3,0},{4,5},{5,6},{6,7},{7,4},{8,9},{9,10},{10,1... | collective-permute-start | bytes 983048 | tf_op jit(solution)/shard_map/ppermute | solution.py:56
  7.2 1.5 collective-permute-start.7
  8.7 0.5 collective-permute-start
  9.2 1.0 copy-done.14
  10.2 0.8 shard_map.170
  11.1 8.7 %all-to-all-start = ((bf16[16,4,3072]{2,1,0:T(4,128)(2,1)}), bf16[16,4,3072]{2,1,0:T(4,128)(2,1)}, u32[]{:S(2)}, u32[]{:S(2)}) async-start(bf16[16,4,3072]{2,1,0:T(4,128)(2,1)} %shard_map.170), calls=%async_computation | async-start | bytes 786432 | tf_op jit(solution)/shard_map/all_to_all | solution.py:567
  19.8 0.9 constant_dynamic-slice_fusion
  20.8 3.3 %collective-permute-start.1 = (bf16[128,1792]{1,0:T(8,128)(2,1)}, bf16[128,1792]{1,0:T(8,128)(2,1)}, u32[]{:S(2)}, u32[]{:S(2)}) collective-permute-start(bf16[128,1792]{1,0:T(8,128)(2,1)} %get-tuple-element.36.refs_0_), channel_id=1, source_target_pairs={{0,1},{1,2},{2,3},{3,0},{4,5},{5,6},{6,7},{7,4},{8,9},{9,10},{10,1... | collective-permute-start | bytes 1376264 | tf_op jit(solution)/shard_map/ppermute | solution.py:56
  24.1 2.1 %collective-permute-done.refs_1_ = bf16[128,1792]{1,0:T(8,128)(2,1)} collective-permute-done((bf16[128,1792]{1,0:T(8,128)(2,1)}, bf16[128,1792]{1,0:T(8,128)(2,1)}, u32[]{:S(2)}, u32[]{:S(2)}) %collective-permute-start) | collective-permute-done | bytes 458784 | tf_op jit(solution)/shard_map/ppermute | solution.py:52
  26.3 0.7 slice.9
  27.0 2.0 %shard_map.163 = bf16[256,1280]{1,0:T(8,128)(2,1)} custom-call(bf16[128,1280]{1,0:T(8,128)(2,1)} %collective-permute-done.8.low.refs_6_.refs_10_, bf16[128,1280]{1,0:T(8,128)(2,1)S(1)} %collective-permute-done.9.high.refs_7_.refs_11_), custom_call_target="tpu_custom_call" | custom-call | flops 10000 | bytes 1310720 | tf_op jit(solution)/shard_map/pallas_call | solution.py:76
  29.0 1.6 slice.8
  30.6 3.2 %collective-permute-start.11 = (bf16[64,1280]{1,0:T(8,128)(2,1)}, bf16[64,1280]{1,0:T(8,128)(2,1)}, u32[]{:S(2)}, u32[]{:S(2)}) collective-permute-start(bf16[64,1280]{1,0:T(8,128)(2,1)} %slice.8), channel_id=1, source_target_pairs={{0,1},{1,2},{2,3},{3,0},{4,5},{5,6},{6,7},{7,4},{8,9},{9,10},{10,1... | collective-permute-start | bytes 491528 | tf_op jit(solution)/shard_map/ppermute | solution.py:56
  33.8 1.5 collective-permute-start.10
  35.3 0.8 multiply_cosine_fusion
  36.1 1.2 subtract_reduce_fusion.mine
  37.4 1.9 %collective-permute-start.3 = (bf16[128,1792]{1,0:T(8,128)(2,1)}, bf16[128,1792]{1,0:T(8,128)(2,1)}, u32[]{:S(2)}, u32[]{:S(2)}) collective-permute-start(bf16[128,1792]{1,0:T(8,128)(2,1)} %collective-permute-done.refs_1_), channel_id=1, source_target_pairs={{0,1},{1,2},{2,3},{3,0},{4,5},{5,6},{6,7},{7,4},{8,9},{9,10},{10,1... | collective-permute-start | bytes 1376264 | tf_op jit(solution)/shard_map/ppermute | solution.py:56
  39.3 2.8 %collective-permute-done.12.high = bf16[64,1280]{1,0:T(8,128)(2,1)} collective-permute-done((bf16[64,1280]{1,0:T(8,128)(2,1)}, bf16[64,1280]{1,0:T(8,128)(2,1)}, u32[]{:S(2)}, u32[]{:S(2)}) %collective-permute-start.12) | collective-permute-done | bytes 163872 | tf_op jit(solution)/shard_map/ppermute | solution.py:60
  42.1 3.0 %collective-permute-start.14 = (f32[4,3072]{1,0:T(4,128)S(1)}, f32[4,3072]{1,0:T(4,128)S(1)}, u32[]{:S(2)}, u32[]{:S(2)}) collective-permute-start(f32[4,3072]{1,0:T(4,128)S(1)} %subtract_reduce_fusion.mine), channel_id=1, source_target_pairs={{0,128},{8,136},{16,144},{24,152},{32,160},{40,168},{48,176},{56,1... | collective-permute-start | bytes 147464 | tf_op jit(solution)/shard_map/ppermute | solution.py:573
  45.1 2.0 %collective-permute-start.6 = (bf16[128,1792]{1,0:T(8,128)(2,1)}, bf16[128,1792]{1,0:T(8,128)(2,1)}, u32[]{:S(2)}, u32[]{:S(2)}) collective-permute-start(bf16[128,1792]{1,0:T(8,128)(2,1)} %collective-permute-done.4.refs_1_.refs_5_), channel_id=1, source_target_pairs={{0,3},{1,0},{2,1},{3,2},{4,7},{5,4},{6,5},{7,6},{8,11},{9,8},{10,9... | collective-permute-start | bytes 1376264 | tf_op jit(solution)/shard_map/ppermute | solution.py:60
  47.2 1.8 %shard_map.164.refs_2_.refs_13_ = bf16[128,1280]{1,0:T(8,128)(2,1)} custom-call(bf16[64,1280]{1,0:T(8,128)(2,1)} %collective-permute-done.11.low, bf16[64,1280]{1,0:T(8,128)(2,1)} %collective-permute-done.12.high), custom_call_target="tpu_custom_call" | custom-call | flops 10000 | bytes 655360 | tf_op jit(solution)/shard_map/pallas_call | solution.py:76
  48.9 3.4 %collective-permute-done.14.other = f32[4,3072]{1,0:T(4,128)S(1)} collective-permute-done((f32[4,3072]{1,0:T(4,128)S(1)}, f32[4,3072]{1,0:T(4,128)S(1)}, u32[]{:S(2)}, u32[]{:S(2)}) %collective-permute-start.14) | collective-permute-done | bytes 49184 | tf_op jit(solution)/shard_map/ppermute | solution.py:573
  52.5 0.8 pad_maximum_fusion
  53.3 3.5 %shard_map.165.first = f32[512,512]{1,0:T(8,128)S(1)} custom-call(bf16[128,1792]{1,0:T(8,128)(2,1)} %get-tuple-element.36.refs_0_, bf16[128,1792]{1,0:T(8,128)(2,1)} %collective-permute-done.refs_1_, bf16[128,1792]{1,0:T(8,128)(2,1)} %collective-permute-done.1.refs_2_, bf16[128,1792]{1,0:T(8,128)(2,1)} %collective-permute-done.2.refs_3_, ...), custom_call_target="tpu_custom_call" | custom-call | flops 1610612736 | bytes 7340032 | tf_op jit(solution)/shard_map/pallas_call | solution.py:76
  56.8 1.0 copy-done.6
  57.9 0.9 copy-done.5
  58.8 8.6 %all-to-all-start.1 = ((f32[16,4,3072]{2,1,0:T(4,128)}), f32[16,4,3072]{2,1,0:T(4,128)}, u32[]{:S(2)}, u32[]{:S(2)}) async-start(f32[16,4,3072]{2,1,0:T(4,128)} %copy-done.5), calls=%async_computation.1 | async-start | bytes 1572864 | tf_op jit(solution)/shard_map/all_to_all | solution.py:577
  67.4 2.3 %shard_map.166.second = f32[256,512]{1,0:T(8,128)S(1)} custom-call(bf16[128,1792]{1,0:T(8,128)(2,1)} %collective-permute-done.3.refs_0_.refs_4_, bf16[128,1792]{1,0:T(8,128)(2,1)} %collective-permute-done.4.refs_1_.refs_5_, bf16[256,1280]{1,0:T(8,128)(2,1)} %collective-permute-done.10.refs_2_.refs_12_, bf16[3072,256]{1,0:T(8,128)(2,1)S(1)} %bitcast.11, ...), custom_call_target="tpu_custom_call" | custom-call | flops 805306368 | bytes 5242880 | tf_op jit(solution)/shard_map/pallas_call | solution.py:76
  69.8 2.4 %shard_map.167.third = f32[256,512]{1,0:T(8,128)S(1)} custom-call(bf16[128,1792]{1,0:T(8,128)(2,1)} %collective-permute-done.5.refs_0_.refs_6_, bf16[128,1792]{1,0:T(8,128)(2,1)} %collective-permute-done.6.refs_1_.refs_7_, bf16[128,1280]{1,0:T(8,128)(2,1)} %shard_map.164.refs_2_.refs_13_, bf16[128,1280]{1,0:T(8,128)(2,1)} %collective-permute-done.13.refs_3_.refs_14_, ...), custom_call_target="tpu_custom_call" | custom-call | flops 805306368 | bytes 5242880 | tf_op jit(solution)/shard_map/pallas_call | solution.py:76
  72.3 8.3 %shard_map.168.refs_15_.grads = bf16[1024,512]{1,0:T(8,128)(2,1)S(1)} custom-call(s32[8]{0:T(128)S(1)} %fusion.at, f32[512,512]{1,0:T(8,128)S(1)} %copy-done.7, f32[256,512]{1,0:T(8,128)S(1)} %shard_map.166.second, f32[256,512]{1,0:T(8,128)S(1)} %shard_map.167.third, f32[64,128]{1,0:T(8,128)S(1)} %get-tuple-element.71.coarse, ...), custom_call_target="tpu_custom_call" | custom-call | flops 2684354560 | bytes 3735584 | tf_op jit(solution)/shard_map/pallas_call | solution.py:76
  80.5 1.6 shard_map.176
  82.1 1.8 %collective-permute-start.18 = (bf16[256,768]{1,0:T(8,128)(2,1)S(1)}, bf16[256,768]{1,0:T(8,128)(2,1)S(1)}, u32[]{:S(2)}, u32[]{:S(2)}) collective-permute-start(bf16[256,768]{1,0:T(8,128)(2,1)S(1)} %get-tuple-element.45), channel_id=1, source_target_pairs={{0,1},{1,2},{2,3},{3,0},{4,5},{5,6},{6,7},{7,4},{8,9},{9,10},{10,1... | collective-permute-start | bytes 1179656 | tf_op jit(solution)/shard_map/ppermute | solution.py:56
  83.9 2.8 %shard_map.177 = (bf16[128,1536]{1,0:T(8,128)(2,1)S(1)}, bf16[256,1536]{1,0:T(8,128)(2,1)S(1)}, bf16[128,1536]{1,0:T(8,128)(2,1)}) custom-call(s32[8]{0:T(128)S(1)} %fusion.at, bf16[1024,512]{1,0:T(8,128)(2,1)S(1)} %shard_map.168.refs_15_.grads, bf16[3072,256]{1,0:T(8,128)(2,1)S(1)} %bitcast.14, bf16[3072,128]{1,0:T(8,128)(2,1)S(1)} %bitcast.21, ...), custom_call_target="tpu_custom_call" | custom-call | flops 805306368 | bytes 5767200 | tf_op jit(solution)/shard_map/pallas_call | solution.py:76
  86.7 0.3 collective-permute-start.19
  87.0 1.9 %collective-permute-start.20 = (bf16[128,1536]{1,0:T(8,128)(2,1)S(1)}, bf16[128,1536]{1,0:T(8,128)(2,1)S(1)}, u32[]{:S(2)}, u32[]{:S(2)}) collective-permute-start(bf16[128,1536]{1,0:T(8,128)(2,1)S(1)} %get-tuple-element.49), channel_id=1, source_target_pairs={{0,4},{1,5},{2,6},{3,7},{4,0},{5,1},{6,2},{7,3},{8,12},{9,13},{10,... | collective-permute-start | bytes 1179656 | tf_op jit(solution)/shard_map/ppermute | solution.py:52
  89.1 3.9 %shard_map.175 = (bf16[256,768]{1,0:T(8,128)(2,1)S(1)}, bf16[256,768]{1,0:T(8,128)(2,1)S(1)}, bf16[256,768]{1,0:T(8,128)(2,1)S(1)}, bf16[256,768]{1,0:T(8,128)(2...) custom-call(s32[8]{0:T(128)S(1)} %fusion.at, ...), custom_call_target="tpu_custom_call" | custom-call | flops 2013265920 | bytes 8126496 | tf_op jit(solution)/shard_map/pallas_call | solution.py:76
  93.0 0.6 collective-permute-done.18.near_low
  93.6 5.5 %collective-permute-done.19.near_high = bf16[256,768]{1,0:T(8,128)(2,1)S(1)} collective-permute-done((bf16[256,768]{1,0:T(8,128)(2,1)S(1)}, bf16[256,768]{1,0:T(8,128)(2,1)S(1)}, u32[]{:S(2)}, u32[]{:S(2)}) %collective-permute-start.19) | collective-permute-done | bytes 393248 | tf_op jit(solution)/shard_map/ppermute | solution.py:60
  99.0 0.3 shard_map.178
  99.3 3.0 %collective-permute-start.21 = (bf16[384,768]{1,0:T(8,128)(2,1)S(1)}, bf16[384,768]{1,0:T(8,128)(2,1)S(1)}, u32[]{:S(2)}, u32[]{:S(2)}) collective-permute-start(bf16[384,768]{1,0:T(8,128)(2,1)S(1)} %get-tuple-element.50), channel_id=1, source_target_pairs={{0,1},{1,2},{2,3},{3,0},{4,5},{5,6},{6,7},{7,4},{8,9},{9,10},{10,1... | collective-permute-start | bytes 1769480 | tf_op jit(solution)/shard_map/ppermute | solution.py:56
  102.3 3.3 %collective-permute-start.23 = (bf16[256,768]{1,0:T(8,128)(2,1)S(1)}, bf16[256,768]{1,0:T(8,128)(2,1)S(1)}, u32[]{:S(2)}, u32[]{:S(2)}) collective-permute-start(bf16[256,768]{1,0:T(8,128)(2,1)S(1)} %get-tuple-element.52), channel_id=1, source_target_pairs={{0,1},{1,2},{2,3},{3,0},{4,5},{5,6},{6,7},{7,4},{8,9},{9,10},{10,1... | collective-permute-start | bytes 1179656 | tf_op jit(solution)/shard_map/ppermute | solution.py:56
  105.6 9.4 %collective-permute-done.27.r = bf16[256,1536]{1,0:T(8,128)(2,1)S(1)} collective-permute-done((bf16[256,1536]{1,0:T(8,128)(2,1)S(1)}, bf16[256,1536]{1,0:T(8,128)(2,1)S(1)}, u32[]{:S(2)}, u32[]{:S(2)}) %collective-permute-start.27) | collective-permute-done | bytes 786464 | tf_op jit(solution)/shard_map/ppermute | solution.py:52
  115.0 1.7 %collective-permute-start.26 = (bf16[128,1536]{1,0:T(8,128)(2,1)}, bf16[128,1536]{1,0:T(8,128)(2,1)}, u32[]{:S(2)}, u32[]{:S(2)}) collective-permute-start(bf16[128,1536]{1,0:T(8,128)(2,1)} %get-tuple-element.57), channel_id=1, source_target_pairs={{0,4},{1,5},{2,6},{3,7},{4,0},{5,1},{6,2},{7,3},{8,12},{9,13},{10,... | collective-permute-start | bytes 1179656 | tf_op jit(solution)/shard_map/ppermute | solution.py:52
  116.7 3.0 %collective-permute-done.24.above_high.near_high = bf16[384,768]{1,0:T(8,128)(2,1)S(1)} collective-permute-done((bf16[384,768]{1,0:T(8,128)(2,1)S(1)}, bf16[384,768]{1,0:T(8,128)(2,1)S(1)}, u32[]{:S(2)}, u32[]{:S(2)}) %collective-permute-start.24) | collective-permute-done | bytes 589856 | tf_op jit(solution)/shard_map/ppermute | solution.py:60
  119.7 1.2 shard_map.180
  120.9 2.0 %collective-permute-start.29 = (bf16[128,1536]{1,0:T(8,128)(2,1)}, bf16[128,1536]{1,0:T(8,128)(2,1)}, u32[]{:S(2)}, u32[]{:S(2)}) collective-permute-start(bf16[128,1536]{1,0:T(8,128)(2,1)} %get-tuple-element.62), channel_id=1, source_target_pairs={{0,3},{1,0},{2,1},{3,2},{4,7},{5,4},{6,5},{7,6},{8,11},{9,8},{10,9... | collective-permute-start | bytes 1179656 | tf_op jit(solution)/shard_map/ppermute | solution.py:60
  123.0 4.2 %collective-permute-done.22.above_low = bf16[256,768]{1,0:T(8,128)(2,1)S(1)} collective-permute-done((bf16[256,768]{1,0:T(8,128)(2,1)S(1)}, bf16[256,768]{1,0:T(8,128)(2,1)S(1)}, u32[]{:S(2)}, u32[]{:S(2)}) %collective-permute-start.22) | collective-permute-done | bytes 393248 | tf_op jit(solution)/shard_map/ppermute | solution.py:60
  127.2 1.0 shard_map.179
  128.2 0.9 copy-done.9
  129.1 2.4 %collective-permute-start.25 = (bf16[128,1536]{1,0:T(8,128)(2,1)}, bf16[128,1536]{1,0:T(8,128)(2,1)}, u32[]{:S(2)}, u32[]{:S(2)}) collective-permute-start(bf16[128,1536]{1,0:T(8,128)(2,1)} %get-tuple-element.55), channel_id=1, source_target_pairs={{0,4},{1,5},{2,6},{3,7},{4,0},{5,1},{6,2},{7,3},{8,12},{9,13},{10,... | collective-permute-start | bytes 1179656 | tf_op jit(solution)/shard_map/ppermute | solution.py:52
  131.5 8.7 %shard_map.169 = (bf16[3072,256]{1,0:T(8,128)(2,1)}, bf16[3072,128]{1,0:T(8,128)(2,1)}, bf16[3072,128]{1,0:T(8,128)(2,1)}, f32[1,3072]{1,0:T(1,128)S(1)}) custom-call(s32[8]{0:T(128)S(1)} %fusion.at, bf16[128,1792]{1,0:T(8,128)(2,1)} %get-tuple-element.36.refs_0_, bf16[128,1792]{1,0:T(8,128)(2,1)} %collective-permute-done.refs_1_, ...), custom_call_target="tpu_custom_call" | custom-call | flops 3221225472 | bytes 13656096 | tf_op jit(solution)/shard_map/pallas_call | solution.py:76
  140.2 3.7 %collective-permute-done.15.arrived = f32[1,3072]{1,0:T(1,128)S(1)} collective-permute-done((f32[1,3072]{1,0:T(1,128)S(1)}, f32[1,3072]{1,0:T(1,128)S(1)}, u32[]{:S(2)}, u32[]{:S(2)}) %collective-permute-start.15) | collective-permute-done | bytes 12320 | tf_op jit(solution)/shard_map/ppermute | solution.py:547
  143.9 3.7 %collective-permute-done.16.arrived = f32[1,3072]{1,0:T(1,128)S(1)} collective-permute-done((f32[1,3072]{1,0:T(1,128)S(1)}, f32[1,3072]{1,0:T(1,128)S(1)}, u32[]{:S(2)}, u32[]{:S(2)}) %collective-permute-start.16) | collective-permute-done | bytes 12320 | tf_op jit(solution)/shard_map/ppermute | solution.py:549
  147.6 5.2 %collective-permute-done.17.other_part = f32[1,3072]{1,0:T(1,128)S(1)} collective-permute-done((f32[1,3072]{1,0:T(1,128)S(1)}, f32[1,3072]{1,0:T(1,128)S(1)}, u32[]{:S(2)}, u32[]{:S(2)}) %collective-permute-start.17) | collective-permute-done | bytes 12320 | tf_op jit(solution)/shard_map/ppermute | solution.py:551
  152.8 1.1 copy-done.8
  154.0 1.1 copy-done.11
  155.1 2.5 %shard_map.174 = (f32[64,3072]{1,0:T(8,128)}, f32[64,3072]{1,0:T(8,128)}, f32[1,3072]{1,0:T(1,128)}) custom-call(f32[16,4,3072]{2,1,0:T(4,128)} %all-to-all-done.1.mean_parts, f32[64,3072]{1,0:T(8,128)S(1)} %copy-done.8, f32[64,3072]{1,0:T(8,128)S(1)} %copy-done.11, f32[1,3072]{1,0:T(1,128)S(1)} %shard_map.173.part, ...), custom_call_target="tpu_custom_call" | custom-call | flops 100000 | bytes 3969024 | tf_op jit(solution)/shard_map/pallas_call | solution.py:76
  157.7 1.1 copy-done.10
  158.8 1.0 copy-done.13
  159.8 3.3 %shard_map.181 = bf16[128,3072]{1,0:T(8,128)(2,1)} custom-call(bf16[128,3072]{1,0:T(8,128)(2,1)S(1)} %bitcast.32, f32[1,3072]{1,0:T(1,128)S(1)} %copy-done.16, f32[128,1536]{1,0:T(8,128)S(1)} %copy-done.10, bf16[128,1536]{1,0:T(8,128)(2,1)} %collective-permute-done.25.from_x, bf16[128,1536]{1,0:T(8,128)(2,1)S(1)} %copy-done.13, ...), custom_call_target="tpu_custom_call" | custom-call | flops 1000000 | bytes 4337664 | tf_op jit(solution)/shard_map/pallas_call | solution.py:76
  (71 shorter events, 0.7 us)
Async XLA Ops:
  0.6 1.1 copy-start.3
  1.8 0.7 copy-start.15
  3.9 16.8 %collective-permute-start.9 = (bf16[128,1280]{1,0:T(8,128)(2,1)}, bf16[128,1280]{1,0:T(8,128)(2,1)S(1)}, u32[]{:S(2)}, u32[]{:S(2)}) collective-permute-start(bf16[128,1280]{1,0:T(8,128)(2,1)} %get-tuple-element.37.refs_4_.refs_8_), channel_id=1, source_target_pairs={{0,3},{1,0},{2,1},{3,2},{4,7},{5,4},{6,5},{7,6},{8,11},{9,8},{10,9... | collective-permute-start | bytes 983048 | tf_op jit(solution)/shard_map/ppermute | solution.py:60
  4.7 22.3 %collective-permute-start.8 = (bf16[128,1280]{1,0:T(8,128)(2,1)}, bf16[128,1280]{1,0:T(8,128)(2,1)}, u32[]{:S(2)}, u32[]{:S(2)}) collective-permute-start(bf16[128,1280]{1,0:T(8,128)(2,1)} %get-tuple-element.37.refs_4_.refs_8_), channel_id=1, source_target_pairs={{0,1},{1,2},{2,3},{3,0},{4,5},{5,6},{6,7},{7,4},{8,9},{9,10},{10,1... | collective-permute-start | bytes 983048 | tf_op jit(solution)/shard_map/ppermute | solution.py:56
  7.2 23.4 %collective-permute-start.7 = (bf16[128,1280]{1,0:T(8,128)(2,1)}, bf16[128,1280]{1,0:T(8,128)(2,1)}, u32[]{:S(2)}, u32[]{:S(2)}) collective-permute-start(bf16[128,1280]{1,0:T(8,128)(2,1)} %get-tuple-element.37.refs_4_.refs_8_), channel_id=1, source_target_pairs={{0,4},{1,5},{2,6},{3,7},{4,0},{5,1},{6,2},{7,3},{8,12},{9,13},{10,... | collective-permute-start | bytes 983048 | tf_op jit(solution)/shard_map/ppermute | solution.py:52
  8.7 25.2 %collective-permute-start.2 = (bf16[128,1792]{1,0:T(8,128)(2,1)}, bf16[128,1792]{1,0:T(8,128)(2,1)}, u32[]{:S(2)}, u32[]{:S(2)}) collective-permute-start(bf16[128,1792]{1,0:T(8,128)(2,1)} %get-tuple-element.36.refs_0_), channel_id=1, source_target_pairs={{0,3},{1,0},{2,1},{3,2},{4,7},{5,4},{6,5},{7,6},{8,11},{9,8},{10,9... | collective-permute-start | bytes 1376264 | tf_op jit(solution)/shard_map/ppermute | solution.py:60
  8.7 17.5 %collective-permute-start = (bf16[128,1792]{1,0:T(8,128)(2,1)}, bf16[128,1792]{1,0:T(8,128)(2,1)}, u32[]{:S(2)}, u32[]{:S(2)}) collective-permute-start(bf16[128,1792]{1,0:T(8,128)(2,1)} %get-tuple-element.36.refs_0_), channel_id=1, source_target_pairs={{0,4},{1,5},{2,6},{3,7},{4,0},{5,1},{6,2},{7,3},{8,12},{9,13},{10,... | collective-permute-start | bytes 1376264 | tf_op jit(solution)/shard_map/ppermute | solution.py:52
  9.2 1.0 copy-start.14
  11.0 36.1 %copy-start.18 = (s32[8]{0:T(128)S(1)}, s32[8]{0:T(128)}, u32[]{:S(2)}) copy-start(s32[8]{0:T(128)} %constant.82.clone) | copy-start | bytes 100
  11.1 36.1 %copy-start.19 = (s32[8]{0:T(128)S(1)}, s32[8]{0:T(128)}, u32[]{:S(2)}) copy-start(s32[8]{0:T(128)} %constant.81.clone) | copy-start | bytes 100
  11.1 25.1 %all-to-all-start = ((bf16[16,4,3072]{2,1,0:T(4,128)(2,1)}), bf16[16,4,3072]{2,1,0:T(4,128)(2,1)}, u32[]{:S(2)}, u32[]{:S(2)}) async-start(bf16[16,4,3072]{2,1,0:T(4,128)(2,1)} %shard_map.170), calls=%async_computation | async-start | bytes 786432 | tf_op jit(solution)/shard_map/all_to_all | solution.py:567
  20.8 16.6 %collective-permute-start.1 = (bf16[128,1792]{1,0:T(8,128)(2,1)}, bf16[128,1792]{1,0:T(8,128)(2,1)}, u32[]{:S(2)}, u32[]{:S(2)}) collective-permute-start(bf16[128,1792]{1,0:T(8,128)(2,1)} %get-tuple-element.36.refs_0_), channel_id=1, source_target_pairs={{0,1},{1,2},{2,3},{3,0},{4,5},{5,6},{6,7},{7,4},{8,9},{9,10},{10,1... | collective-permute-start | bytes 1376264 | tf_op jit(solution)/shard_map/ppermute | solution.py:56
  26.2 18.9 %collective-permute-start.4 = (bf16[128,1792]{1,0:T(8,128)(2,1)}, bf16[128,1792]{1,0:T(8,128)(2,1)}, u32[]{:S(2)}, u32[]{:S(2)}) collective-permute-start(bf16[128,1792]{1,0:T(8,128)(2,1)} %collective-permute-done.refs_1_), channel_id=1, source_target_pairs={{0,3},{1,0},{2,1},{3,2},{4,7},{5,4},{6,5},{7,6},{8,11},{9,8},{10,9... | collective-permute-start | bytes 1376264 | tf_op jit(solution)/shard_map/ppermute | solution.py:60
  26.3 27.0 %copy-start.2 = (bf16[1,3072,128]{2,1,0:T(8,128)(2,1)S(1)}, bf16[1,3072,128]{2,1,0:T(8,128)(2,1)}, u32[]{:S(2)}) copy-start(bf16[1,3072,128]{2,1,0:T(8,128)(2,1)} %param.15) | copy-start | bytes 2359300
  27.0 26.3 %copy-start = (bf16[1,3072,256]{2,1,0:T(8,128)(2,1)S(1)}, bf16[1,3072,256]{2,1,0:T(8,128)(2,1)}, u32[]{:S(2)}) copy-start(bf16[1,3072,256]{2,1,0:T(8,128)(2,1)} %param.13) | copy-start | bytes 4718596
  27.0 26.3 %copy-start.1 = (bf16[1,3072,128]{2,1,0:T(8,128)(2,1)S(1)}, bf16[1,3072,128]{2,1,0:T(8,128)(2,1)}, u32[]{:S(2)}) copy-start(bf16[1,3072,128]{2,1,0:T(8,128)(2,1)} %param.14) | copy-start | bytes 2359300
  27.0 15.1 %collective-permute-start.12 = (bf16[64,1280]{1,0:T(8,128)(2,1)}, bf16[64,1280]{1,0:T(8,128)(2,1)}, u32[]{:S(2)}, u32[]{:S(2)}) collective-permute-start(bf16[64,1280]{1,0:T(8,128)(2,1)} %slice.9), channel_id=1, source_target_pairs={{0,3},{1,0},{2,1},{3,2},{4,7},{5,4},{6,5},{7,6},{8,11},{9,8},{10,9... | collective-permute-start | bytes 491528 | tf_op jit(solution)/shard_map/ppermute | solution.py:60
  30.6 11.5 %collective-permute-start.11 = (bf16[64,1280]{1,0:T(8,128)(2,1)}, bf16[64,1280]{1,0:T(8,128)(2,1)}, u32[]{:S(2)}, u32[]{:S(2)}) collective-permute-start(bf16[64,1280]{1,0:T(8,128)(2,1)} %slice.8), channel_id=1, source_target_pairs={{0,1},{1,2},{2,3},{3,0},{4,5},{5,6},{6,7},{7,4},{8,9},{9,10},{10,1... | collective-permute-start | bytes 491528 | tf_op jit(solution)/shard_map/ppermute | solution.py:56
  33.8 33.6 %collective-permute-start.10 = (bf16[256,1280]{1,0:T(8,128)(2,1)}, bf16[256,1280]{1,0:T(8,128)(2,1)}, u32[]{:S(2)}, u32[]{:S(2)}) collective-permute-start(bf16[256,1280]{1,0:T(8,128)(2,1)} %shard_map.163), channel_id=1, source_target_pairs={{0,4},{1,5},{2,6},{3,7},{4,0},{5,1},{6,2},{7,3},{8,12},{9,13},{10,... | collective-permute-start | bytes 1966088 | tf_op jit(solution)/shard_map/ppermute | solution.py:52
  37.4 30.0 %collective-permute-start.3 = (bf16[128,1792]{1,0:T(8,128)(2,1)}, bf16[128,1792]{1,0:T(8,128)(2,1)}, u32[]{:S(2)}, u32[]{:S(2)}) collective-permute-start(bf16[128,1792]{1,0:T(8,128)(2,1)} %collective-permute-done.refs_1_), channel_id=1, source_target_pairs={{0,1},{1,2},{2,3},{3,0},{4,5},{5,6},{6,7},{7,4},{8,9},{9,10},{10,1... | collective-permute-start | bytes 1376264 | tf_op jit(solution)/shard_map/ppermute | solution.py:56
  42.1 27.7 %collective-permute-start.5 = (bf16[128,1792]{1,0:T(8,128)(2,1)}, bf16[128,1792]{1,0:T(8,128)(2,1)}, u32[]{:S(2)}, u32[]{:S(2)}) collective-permute-start(bf16[128,1792]{1,0:T(8,128)(2,1)} %collective-permute-done.1.refs_2_), channel_id=1, source_target_pairs={{0,1},{1,2},{2,3},{3,0},{4,5},{5,6},{6,7},{7,4},{8,9},{9,10},{10,1... | collective-permute-start | bytes 1376264 | tf_op jit(solution)/shard_map/ppermute | solution.py:56
  42.1 10.3 %collective-permute-start.14 = (f32[4,3072]{1,0:T(4,128)S(1)}, f32[4,3072]{1,0:T(4,128)S(1)}, u32[]{:S(2)}, u32[]{:S(2)}) collective-permute-start(f32[4,3072]{1,0:T(4,128)S(1)} %subtract_reduce_fusion.mine), channel_id=1, source_target_pairs={{0,128},{8,136},{16,144},{24,152},{32,160},{40,168},{48,176},{56,1... | collective-permute-start | bytes 147464 | tf_op jit(solution)/shard_map/ppermute | solution.py:573
  45.1 24.7 %collective-permute-start.6 = (bf16[128,1792]{1,0:T(8,128)(2,1)}, bf16[128,1792]{1,0:T(8,128)(2,1)}, u32[]{:S(2)}, u32[]{:S(2)}) collective-permute-start(bf16[128,1792]{1,0:T(8,128)(2,1)} %collective-permute-done.4.refs_1_.refs_5_), channel_id=1, source_target_pairs={{0,3},{1,0},{2,1},{3,2},{4,7},{5,4},{6,5},{7,6},{8,11},{9,8},{10,9... | collective-permute-start | bytes 1376264 | tf_op jit(solution)/shard_map/ppermute | solution.py:60
  52.4 17.4 %collective-permute-start.13 = (bf16[128,1280]{1,0:T(8,128)(2,1)}, bf16[128,1280]{1,0:T(8,128)(2,1)}, u32[]{:S(2)}, u32[]{:S(2)}) collective-permute-start(bf16[128,1280]{1,0:T(8,128)(2,1)} %shard_map.164.refs_2_.refs_13_), channel_id=1, source_target_pairs={{0,4},{1,5},{2,6},{3,7},{4,0},{5,1},{6,2},{7,3},{8,12},{9,13},{10,... | collective-permute-start | bytes 983048 | tf_op jit(solution)/shard_map/ppermute | solution.py:52
  56.8 1.0 copy-start.6
  57.9 0.9 copy-start.5
  58.8 94.0 %all-to-all-start.1 = ((f32[16,4,3072]{2,1,0:T(4,128)}), f32[16,4,3072]{2,1,0:T(4,128)}, u32[]{:S(2)}, u32[]{:S(2)}) async-start(f32[16,4,3072]{2,1,0:T(4,128)} %copy-done.5), calls=%async_computation.1 | async-start | bytes 1572864 | tf_op jit(solution)/shard_map/all_to_all | solution.py:577
  69.8 2.5 %copy-start.7 = (f32[512,512]{1,0:T(8,128)S(1)}, f32[512,512]{1,0:T(8,128)}, u32[]{:S(2)}) copy-start(f32[512,512]{1,0:T(8,128)} %copy-done.6) | copy-start | bytes 3145732
  69.8 2.5 %copy-start.17 = (bf16[1,1024,256]{2,1,0:T(8,128)(2,1)S(1)}, bf16[1,1024,256]{2,1,0:T(8,128)(2,1)}, u32[]{:S(2)}) copy-start(bf16[1,1024,256]{2,1,0:T(8,128)(2,1)} %param.16) | copy-start | bytes 1572868
  82.1 11.5 %collective-permute-start.18 = (bf16[256,768]{1,0:T(8,128)(2,1)S(1)}, bf16[256,768]{1,0:T(8,128)(2,1)S(1)}, u32[]{:S(2)}, u32[]{:S(2)}) collective-permute-start(bf16[256,768]{1,0:T(8,128)(2,1)S(1)} %get-tuple-element.45), channel_id=1, source_target_pairs={{0,1},{1,2},{2,3},{3,0},{4,5},{5,6},{6,7},{7,4},{8,9},{9,10},{10,1... | collective-permute-start | bytes 1179656 | tf_op jit(solution)/shard_map/ppermute | solution.py:56
  86.7 12.3 %collective-permute-start.19 = (bf16[256,768]{1,0:T(8,128)(2,1)S(1)}, bf16[256,768]{1,0:T(8,128)(2,1)S(1)}, u32[]{:S(2)}, u32[]{:S(2)}) collective-permute-start(bf16[256,768]{1,0:T(8,128)(2,1)S(1)} %get-tuple-element.47), channel_id=1, source_target_pairs={{0,3},{1,0},{2,1},{3,2},{4,7},{5,4},{6,5},{7,6},{8,11},{9,8},{10,9... | collective-permute-start | bytes 1179656 | tf_op jit(solution)/shard_map/ppermute | solution.py:60
  87.0 12.0 %collective-permute-start.20 = (bf16[128,1536]{1,0:T(8,128)(2,1)S(1)}, bf16[128,1536]{1,0:T(8,128)(2,1)S(1)}, u32[]{:S(2)}, u32[]{:S(2)}) collective-permute-start(bf16[128,1536]{1,0:T(8,128)(2,1)S(1)} %get-tuple-element.49), channel_id=1, source_target_pairs={{0,4},{1,5},{2,6},{3,7},{4,0},{5,1},{6,2},{7,3},{8,12},{9,13},{10,... | collective-permute-start | bytes 1179656 | tf_op jit(solution)/shard_map/ppermute | solution.py:52
  88.9 26.1 %collective-permute-start.27 = (bf16[256,1536]{1,0:T(8,128)(2,1)S(1)}, bf16[256,1536]{1,0:T(8,128)(2,1)S(1)}, u32[]{:S(2)}, u32[]{:S(2)}) collective-permute-start(bf16[256,1536]{1,0:T(8,128)(2,1)S(1)} %get-tuple-element.60), channel_id=1, source_target_pairs={{0,4},{1,5},{2,6},{3,7},{4,0},{5,1},{6,2},{7,3},{8,12},{9,13},{10,... | collective-permute-start | bytes 2359304 | tf_op jit(solution)/shard_map/ppermute | solution.py:52
  93.0 28.0 %copy-start.12 = (bf16[128,1536]{1,0:T(8,128)(2,1)}, bf16[128,1536]{1,0:T(8,128)(2,1)S(1)}, u32[]{:S(2)}) copy-start(bf16[128,1536]{1,0:T(8,128)(2,1)S(1)} %get-tuple-element.56.q0) | copy-start | bytes 1179652
  99.3 17.4 %collective-permute-start.21 = (bf16[384,768]{1,0:T(8,128)(2,1)S(1)}, bf16[384,768]{1,0:T(8,128)(2,1)S(1)}, u32[]{:S(2)}, u32[]{:S(2)}) collective-permute-start(bf16[384,768]{1,0:T(8,128)(2,1)S(1)} %get-tuple-element.50), channel_id=1, source_target_pairs={{0,1},{1,2},{2,3},{3,0},{4,5},{5,6},{6,7},{7,4},{8,9},{9,10},{10,1... | collective-permute-start | bytes 1769480 | tf_op jit(solution)/shard_map/ppermute | solution.py:56
  102.3 17.4 %collective-permute-start.24 = (bf16[384,768]{1,0:T(8,128)(2,1)S(1)}, bf16[384,768]{1,0:T(8,128)(2,1)S(1)}, u32[]{:S(2)}, u32[]{:S(2)}) collective-permute-start(bf16[384,768]{1,0:T(8,128)(2,1)S(1)} %get-tuple-element.53), channel_id=1, source_target_pairs={{0,3},{1,0},{2,1},{3,2},{4,7},{5,4},{6,5},{7,6},{8,11},{9,8},{10,9... | collective-permute-start | bytes 1769480 | tf_op jit(solution)/shard_map/ppermute | solution.py:60
  102.3 24.9 %collective-permute-start.22 = (bf16[256,768]{1,0:T(8,128)(2,1)S(1)}, bf16[256,768]{1,0:T(8,128)(2,1)S(1)}, u32[]{:S(2)}, u32[]{:S(2)}) collective-permute-start(bf16[256,768]{1,0:T(8,128)(2,1)S(1)} %get-tuple-element.51), channel_id=1, source_target_pairs={{0,3},{1,0},{2,1},{3,2},{4,7},{5,4},{6,5},{7,6},{8,11},{9,8},{10,9... | collective-permute-start | bytes 1179656 | tf_op jit(solution)/shard_map/ppermute | solution.py:60
  102.3 24.9 %collective-permute-start.23 = (bf16[256,768]{1,0:T(8,128)(2,1)S(1)}, bf16[256,768]{1,0:T(8,128)(2,1)S(1)}, u32[]{:S(2)}, u32[]{:S(2)}) collective-permute-start(bf16[256,768]{1,0:T(8,128)(2,1)S(1)} %get-tuple-element.52), channel_id=1, source_target_pairs={{0,1},{1,2},{2,3},{3,0},{4,5},{5,6},{6,7},{7,4},{8,9},{9,10},{10,1... | collective-permute-start | bytes 1179656 | tf_op jit(solution)/shard_map/ppermute | solution.py:56
  115.0 42.7 %collective-permute-start.26 = (bf16[128,1536]{1,0:T(8,128)(2,1)}, bf16[128,1536]{1,0:T(8,128)(2,1)}, u32[]{:S(2)}, u32[]{:S(2)}) collective-permute-start(bf16[128,1536]{1,0:T(8,128)(2,1)} %get-tuple-element.57), channel_id=1, source_target_pairs={{0,4},{1,5},{2,6},{3,7},{4,0},{5,1},{6,2},{7,3},{8,12},{9,13},{10,... | collective-permute-start | bytes 1179656 | tf_op jit(solution)/shard_map/ppermute | solution.py:52
  120.9 10.5 %copy-start.16 = (f32[1,3072]{1,0:T(1,128)S(1)}, f32[1,3072]{1,0:T(1,128)}, u32[]{:S(2)}) copy-start(f32[1,3072]{1,0:T(1,128)} %gain.3) | copy-start | bytes 36868
  120.9 36.7 %collective-permute-start.28 = (bf16[128,1536]{1,0:T(8,128)(2,1)}, bf16[128,1536]{1,0:T(8,128)(2,1)}, u32[]{:S(2)}, u32[]{:S(2)}) collective-permute-start(bf16[128,1536]{1,0:T(8,128)(2,1)} %get-tuple-element.61), channel_id=1, source_target_pairs={{0,1},{1,2},{2,3},{3,0},{4,5},{5,6},{6,7},{7,4},{8,9},{9,10},{10,1... | collective-permute-start | bytes 1179656 | tf_op jit(solution)/shard_map/ppermute | solution.py:56
  120.9 36.7 %collective-permute-start.29 = (bf16[128,1536]{1,0:T(8,128)(2,1)}, bf16[128,1536]{1,0:T(8,128)(2,1)}, u32[]{:S(2)}, u32[]{:S(2)}) collective-permute-start(bf16[128,1536]{1,0:T(8,128)(2,1)} %get-tuple-element.62), channel_id=1, source_target_pairs={{0,3},{1,0},{2,1},{3,2},{4,7},{5,4},{6,5},{7,6},{8,11},{9,8},{10,9... | collective-permute-start | bytes 1179656 | tf_op jit(solution)/shard_map/ppermute | solution.py:60
  128.2 0.9 copy-start.9
  129.1 28.6 %collective-permute-start.25 = (bf16[128,1536]{1,0:T(8,128)(2,1)}, bf16[128,1536]{1,0:T(8,128)(2,1)}, u32[]{:S(2)}, u32[]{:S(2)}) collective-permute-start(bf16[128,1536]{1,0:T(8,128)(2,1)} %get-tuple-element.55), channel_id=1, source_target_pairs={{0,4},{1,5},{2,6},{3,7},{4,0},{5,1},{6,2},{7,3},{8,12},{9,13},{10,... | collective-permute-start | bytes 1179656 | tf_op jit(solution)/shard_map/ppermute | solution.py:52
  140.2 17.5 %copy-start.4 = (bf16[1,128,3072]{2,1,0:T(8,128)(2,1)S(1)}, bf16[1,128,3072]{2,1,0:T(8,128)(2,1)}, u32[]{:S(2)}) copy-start(bf16[1,128,3072]{2,1,0:T(8,128)(2,1)} %param.11) | copy-start | bytes 2359300
  140.2 3.7 %collective-permute-start.15 = (f32[1,3072]{1,0:T(1,128)S(1)}, f32[1,3072]{1,0:T(1,128)S(1)}, u32[]{:S(2)}, u32[]{:S(2)}) collective-permute-start(f32[1,3072]{1,0:T(1,128)S(1)} %get-tuple-element.41.mine), channel_id=1, source_target_pairs={{0,4},{1,5},{2,6},{3,7},{4,0},{5,1},{6,2},{7,3},{8,12},{9,13},{10,... | collective-permute-start | bytes 36872 | tf_op jit(solution)/shard_map/ppermute | solution.py:547
  143.9 3.7 %collective-permute-start.16 = (f32[1,3072]{1,0:T(1,128)S(1)}, f32[1,3072]{1,0:T(1,128)S(1)}, u32[]{:S(2)}, u32[]{:S(2)}) collective-permute-start(f32[1,3072]{1,0:T(1,128)S(1)} %shard_map.172.mine), channel_id=1, source_target_pairs={{0,1},{1,0},{2,3},{3,2},{4,5},{5,4},{6,7},{7,6},{8,9},{9,8},{10,11... | collective-permute-start | bytes 36872 | tf_op jit(solution)/shard_map/ppermute | solution.py:549
  147.6 5.2 %collective-permute-start.17 = (f32[1,3072]{1,0:T(1,128)S(1)}, f32[1,3072]{1,0:T(1,128)S(1)}, u32[]{:S(2)}, u32[]{:S(2)}) collective-permute-start(f32[1,3072]{1,0:T(1,128)S(1)} %shard_map.173.part), channel_id=1, source_target_pairs={{0,2},{1,3},{2,0},{3,1},{4,6},{5,7},{6,4},{7,5},{8,10},{9,11},{10,... | collective-permute-start | bytes 36872 | tf_op jit(solution)/shard_map/ppermute | solution.py:551
  152.8 1.1 copy-start.8
  154.0 1.1 copy-start.11
  157.7 1.1 copy-start.10
  158.8 1.0 copy-start.13
where the time goes:
time: 164 us; the launch traced here: 163 us
  starting transfers between devices  54.4 us (33%)
  Pallas kernels  48.1 us (29%)
  waiting for transfers between devices  43.7 us (27%)
  local copies, waits for them, and re-layouts  13.2 us (8%)
  other arithmetic  2.9 us (2%)
    pallas_call x20, Pallas kernels, call(): pl.pallas_call(kernel, out_shape=tuple(outs), in_specs=[SM] * smem + [VM]...  48.1 us
    ppermute x9, starting transfers between devices, up(): return lax.ppermute(value, 'tp', UP_PAIRS)  19 us
    ppermute x9, waiting for transfers between devices, down(): return lax.ppermute(value, 'tp', DOWN_PAIRS)  15.5 us
    ppermute x8, waiting for transfers between devices, across(): return lax.ppermute(value, 'tp', X_PAIRS)  11.5 us
    unnamed x40, local copies, waits for them, and re-layouts  9.98 us
    ppermute x8, starting transfers between devices, across(): return lax.ppermute(value, 'tp', X_PAIRS)  9.82 us
    all_to_all x1, starting transfers between devices, body(): lax.all_to_all(parts, 'rep', split_axis=0, concat_axis=0, tiled=True, axi...  8.75 us
    all_to_all x1, starting transfers between devices, body(): lax.all_to_all(copies, 'rep', split_axis=0, concat_axis=0, tiled=True, ax...  8.61 us
  transfers between devices with their start and end apart: 32, of which 11 were waited for; matrix products, arithmetic and copies ran while one was open for 4% of the time, Pallas kernels for 27%

commit v1 on v0

--- a/solution.py
+++ b/solution.py
@@ -261,7 +261,7 @@
 
 def weight_kernel(at, *refs):
     parts_a, parts_b = refs[:8], refs[8:15]
-    grads, wq, wk, wv, gain, dwq, dwk, dwv, gain_part, ordered = refs[15:]
+    grads, wq, wk, wv, dwq, dwk, dwv, gain_part, ordered = refs[15:]
     for j in range(8):
         ordered[j * ROWS : (j + 1) * ROWS, :] = grads[
             pl.ds(pl.multiple_of(at[j] * ROWS, ROWS), ROWS), :
@@ -279,7 +279,7 @@
             + product[:, 256:384] * wk[where, :].astype(f32)
             + product[:, 384:] * wv[where, :].astype(f32)
         )
-        gain_part[:, where] = jnp.sum(total.T, axis=0, keepdims=True) / gain[:, where]
+        gain_part[:, where] = jnp.sum(total.T, axis=0, keepdims=True)
 
     @pl.loop(0, A // STEP_A)
     def _(i):
@@ -349,7 +349,11 @@
     out[...] = mine[...] + arrived[...]
 
 
-def token_kernel(tokens, gain, own_a, from_x, q0, r0, from_below, from_above, out):
+def token_kernel(
+    tokens, gain, own_a, from_x, q0, r0, from_below, from_above, part, other_part, out, grad_gain
+):
+    grad_gain[...] = (part[...] + other_part[...]) / gain[...]
+
     def body(at):
         wide = tokens[at, :].astype(f32)
         inverse = lax.rsqrt(jnp.mean(wide * wide, axis=-1, keepdims=True) + epsilon)
@@ -370,10 +374,7 @@
     each_block(ROWS, body)
 
 
-def outer_kernel(
-    mean_parts, fragment, momentum, part, other_part, new_fragment, new_momentum, grad_gain
-):
-    grad_gain[...] = part[...] + other_part[...]
+def outer_kernel(mean_parts, fragment, momentum, new_fragment, new_momentum):
     count = mean_parts.shape[1]
 
     @pl.loop(0, mean_parts.shape[0] // 2)
@@ -538,7 +539,7 @@
         weight_kernel,
         "weights",
         [shape(MODEL, 256), shape(MODEL, 128), shape(MODEL, 128), shape(1, MODEL, dtype=f32)],
-        [at] + parts_a + parts_b + [grads] + weights + [norm_gain],
+        [at] + parts_a + parts_b + [grads] + weights,
         2 * SEQ * 512 * MODEL,
         scratch=[pltpu.VMEM((SEQ, 512), bf16)],
         smem=1,
@@ -549,11 +550,12 @@
     arrived_gain = lax.ppermute(gain_part, "tp", swapped(1))
     (gain_part,) = call(gain_sum_kernel, "e_sum1", gain_row, [gain_part, arrived_gain], 10**4)
     arrived_gain = lax.ppermute(gain_part, "tp", swapped(2))
-    (grad_rows,) = call(
+    grad_rows, grad_gain = call(
         token_kernel,
         "tokens",
-        [shape(ROWS, MODEL)],
-        [rows, norm_gain, own_sum, from_x, q0, r0, from_below, from_above],
+        [shape(ROWS, MODEL)] + gain_row,
+        [rows, norm_gain, own_sum, from_x, q0, r0, from_below, from_above]
+        + [gain_part, arrived_gain],
         10**6,
     )
 
@@ -577,11 +579,11 @@
     mean = lax.all_to_all(
         copies, "rep", split_axis=0, concat_axis=0, tiled=True, axis_index_groups=groups
     )
-    new_global, new_momentum, grad_gain = call(
+    new_global, new_momentum = call(
         outer_kernel,
         "outer",
-        [shape(*momentum.shape, dtype=f32)] * 2 + gain_row,
-        [mean, global_fragment, momentum, gain_part, arrived_gain],
+        [shape(*momentum.shape, dtype=f32)] * 2,
+        [mean, global_fragment, momentum],
         10**5,
     )
     return (

time: 164 us -> 167 us (1.018)
  the two profiles are of different devices: /device:TPU:24 before, /device:TPU:4 now
where the time goes in v1:
time: 167 us; the launch traced here: 164 us
  starting transfers between devices  56.5 us (34%)
  Pallas kernels  48.1 us (29%)
  waiting for transfers between devices  42.4 us (25%)
  local copies, waits for them, and re-layouts  13.4 us (8%)
  other arithmetic  2.9 us (2%)
    pallas_call x20, Pallas kernels, call(): pl.pallas_call(kernel, out_shape=tuple(outs), in_specs=[SM] * smem + [VM]...  48.1 us
    ppermute x9, waiting for transfers between devices, down(): return lax.ppermute(value, 'tp', DOWN_PAIRS)  28.8 us
    ppermute x9, starting transfers between devices, down(): return lax.ppermute(value, 'tp', DOWN_PAIRS)  18.9 us
    unnamed x40, local copies, waits for them, and re-layouts  10.2 us
    all_to_all x1, starting transfers between devices, body(): lax.all_to_all(parts, 'rep', split_axis=0, concat_axis=0, tiled=True, axi...  8.75 us
    all_to_all x1, starting transfers between devices, body(): lax.all_to_all(copies, 'rep', split_axis=0, concat_axis=0, tiled=True, ax...  8.61 us
    ppermute x8, starting transfers between devices, across(): return lax.ppermute(value, 'tp', X_PAIRS)  8.42 us
    ppermute x9, starting transfers between devices, up(): return lax.ppermute(value, 'tp', UP_PAIRS)  8 us
  transfers between devices with their start and end apart: 32, of which 11 were waited for; matrix products, arithmetic and copies ran while one was open for 4% of the time, Pallas kernels for 26%

profile of v1, /device:TPU:4, one launch (start us, length us, event | category | flops | bytes accessed | tf_op | source)
XLA Modules:
  0.0 164.3 jit_solution(15901603370951569404)
XLA Ops:
  0.6 1.1 copy-done.4
  1.8 0.7 copy-done.15
  2.5 1.5 shard_map.162
  3.9 1.2 collective-permute-start
  5.1 1.6 collective-permute-start.1
  6.7 0.8 collective-permute-start.7
  7.5 1.6 collective-permute-start.8
  9.1 1.7 %collective-permute-start.9 = (bf16[128,1280]{1,0:T(8,128)(2,1)}, bf16[128,1280]{1,0:T(8,128)(2,1)}, u32[]{:S(2)}, u32[]{:S(2)}) collective-permute-start(bf16[128,1280]{1,0:T(8,128)(2,1)} %get-tuple-element.38.refs_4_.refs_8_), channel_id=1, source_target_pairs={{0,3},{1,0},{2,1},{3,2},{4,7},{5,4},{6,5},{7,6},{8,11},{9,8},{10,9... | collective-permute-start | bytes 983048 | tf_op jit(solution)/shard_map/ppermute | solution.py:60
  10.8 1.0 copy-done.12
  11.8 0.8 shard_map.179
  12.6 8.7 %all-to-all-start = ((bf16[16,4,3072]{2,1,0:T(4,128)(2,1)}), bf16[16,4,3072]{2,1,0:T(4,128)(2,1)}, u32[]{:S(2)}, u32[]{:S(2)}) async-start(bf16[16,4,3072]{2,1,0:T(4,128)(2,1)} %shard_map.179), calls=%async_computation | async-start | bytes 786432 | tf_op jit(solution)/shard_map/all_to_all | solution.py:569
  21.4 0.9 constant_dynamic-slice_fusion
  22.4 3.3 %collective-permute-done.8.low.refs_6_.refs_10_ = bf16[128,1280]{1,0:T(8,128)(2,1)S(1)} collective-permute-done((bf16[128,1280]{1,0:T(8,128)(2,1)}, bf16[128,1280]{1,0:T(8,128)(2,1)S(1)}, u32[]{:S(2)}, u32[]{:S(2)}) %collective-permute-start.8) | collective-permute-done | bytes 327712 | tf_op jit(solution)/shard_map/ppermute | solution.py:56
  25.7 1.7 %collective-permute-start.2 = (bf16[128,1792]{1,0:T(8,128)(2,1)}, bf16[128,1792]{1,0:T(8,128)(2,1)}, u32[]{:S(2)}, u32[]{:S(2)}) collective-permute-start(bf16[128,1792]{1,0:T(8,128)(2,1)} %get-tuple-element.37.refs_0_), channel_id=1, source_target_pairs={{0,3},{1,0},{2,1},{3,2},{4,7},{5,4},{6,5},{7,6},{8,11},{9,8},{10,9... | collective-permute-start | bytes 1376264 | tf_op jit(solution)/shard_map/ppermute | solution.py:60
  27.4 0.7 collective-permute-start.4
  28.2 2.0 %shard_map.163 = bf16[256,1280]{1,0:T(8,128)(2,1)} custom-call(bf16[128,1280]{1,0:T(8,128)(2,1)S(1)} %collective-permute-done.8.low.refs_6_.refs_10_, bf16[128,1280]{1,0:T(8,128)(2,1)} %collective-permute-done.9.high.refs_7_.refs_11_), custom_call_target="tpu_custom_call" | custom-call | flops 10000 | bytes 1310720 | tf_op jit(solution)/shard_map/pallas_call | solution.py:76
  30.2 0.8 collective-permute-start.10
  31.7 1.6 slice.9
  33.3 1.3 collective-permute-start.11
  34.6 2.0 %collective-permute-start.12 = (bf16[64,1280]{1,0:T(8,128)(2,1)}, bf16[64,1280]{1,0:T(8,128)(2,1)}, u32[]{:S(2)}, u32[]{:S(2)}) collective-permute-start(bf16[64,1280]{1,0:T(8,128)(2,1)} %slice.9), channel_id=1, source_target_pairs={{0,3},{1,0},{2,1},{3,2},{4,7},{5,4},{6,5},{7,6},{8,11},{9,8},{10,9... | collective-permute-start | bytes 491528 | tf_op jit(solution)/shard_map/ppermute | solution.py:60
  36.6 0.8 multiply_cosine_fusion
  37.4 1.2 subtract_reduce_fusion.mine
  38.6 0.8 collective-permute-done.2.refs_3_
  40.2 1.1 collective-permute-start.5
  41.2 9.3 %collective-permute-done.12.high = bf16[64,1280]{1,0:T(8,128)(2,1)} collective-permute-done((bf16[64,1280]{1,0:T(8,128)(2,1)}, bf16[64,1280]{1,0:T(8,128)(2,1)}, u32[]{:S(2)}, u32[]{:S(2)}) %collective-permute-start.12) | collective-permute-done | bytes 163872 | tf_op jit(solution)/shard_map/ppermute | solution.py:60
  51.1 3.2 %collective-permute-start.6 = (bf16[128,1792]{1,0:T(8,128)(2,1)}, bf16[128,1792]{1,0:T(8,128)(2,1)}, u32[]{:S(2)}, u32[]{:S(2)}) collective-permute-start(bf16[128,1792]{1,0:T(8,128)(2,1)} %collective-permute-done.4.refs_1_.refs_5_), channel_id=1, source_target_pairs={{0,3},{1,0},{2,1},{3,2},{4,7},{5,4},{6,5},{7,6},{8,11},{9,8},{10,9... | collective-permute-start | bytes 1376264 | tf_op jit(solution)/shard_map/ppermute | solution.py:60
  54.3 1.8 %shard_map.164.refs_2_.refs_13_ = bf16[128,1280]{1,0:T(8,128)(2,1)} custom-call(bf16[64,1280]{1,0:T(8,128)(2,1)} %collective-permute-done.11.low, bf16[64,1280]{1,0:T(8,128)(2,1)} %collective-permute-done.12.high), custom_call_target="tpu_custom_call" | custom-call | flops 10000 | bytes 655360 | tf_op jit(solution)/shard_map/pallas_call | solution.py:76
  56.1 1.1 collective-permute-start.13
  57.2 0.8 pad_maximum_fusion
  58.0 3.5 %shard_map.165.first = f32[512,512]{1,0:T(8,128)S(1)} custom-call(bf16[128,1792]{1,0:T(8,128)(2,1)} %get-tuple-element.37.refs_0_, bf16[128,1792]{1,0:T(8,128)(2,1)} %collective-permute-done.refs_1_, bf16[128,1792]{1,0:T(8,128)(2,1)} %collective-permute-done.1.refs_2_, bf16[128,1792]{1,0:T(8,128)(2,1)} %collective-permute-done.2.refs_3_, ...), custom_call_target="tpu_custom_call" | custom-call | flops 1610612736 | bytes 7340032 | tf_op jit(solution)/shard_map/pallas_call | solution.py:76
  61.5 1.0 copy-done.6
  62.6 0.9 copy-done.3
  63.5 8.6 %all-to-all-start.1 = ((f32[16,4,3072]{2,1,0:T(4,128)}), f32[16,4,3072]{2,1,0:T(4,128)}, u32[]{:S(2)}, u32[]{:S(2)}) async-start(f32[16,4,3072]{2,1,0:T(4,128)} %copy-done.3), calls=%async_computation.1 | async-start | bytes 1572864 | tf_op jit(solution)/shard_map/all_to_all | solution.py:579
  72.1 2.3 %shard_map.166.second = f32[256,512]{1,0:T(8,128)S(1)} custom-call(bf16[128,1792]{1,0:T(8,128)(2,1)} %collective-permute-done.3.refs_0_.refs_4_, bf16[128,1792]{1,0:T(8,128)(2,1)} %collective-permute-done.4.refs_1_.refs_5_, bf16[256,1280]{1,0:T(8,128)(2,1)} %collective-permute-done.10.refs_2_.refs_12_, bf16[3072,256]{1,0:T(8,128)(2,1)S(1)} %bitcast.11, ...), custom_call_target="tpu_custom_call" | custom-call | flops 805306368 | bytes 5242880 | tf_op jit(solution)/shard_map/pallas_call | solution.py:76
  74.5 2.4 %shard_map.167.third = f32[256,512]{1,0:T(8,128)S(1)} custom-call(bf16[128,1792]{1,0:T(8,128)(2,1)} %collective-permute-done.5.refs_0_.refs_6_, bf16[128,1792]{1,0:T(8,128)(2,1)} %collective-permute-done.6.refs_1_.refs_7_, bf16[128,1280]{1,0:T(8,128)(2,1)} %shard_map.164.refs_2_.refs_13_, bf16[128,1280]{1,0:T(8,128)(2,1)} %collective-permute-done.13.refs_3_.refs_14_, ...), custom_call_target="tpu_custom_call" | custom-call | flops 805306368 | bytes 5242880 | tf_op jit(solution)/shard_map/pallas_call | solution.py:76
  77.0 8.3 %shard_map.168.refs_15_.grads = bf16[1024,512]{1,0:T(8,128)(2,1)S(1)} custom-call(s32[8]{0:T(128)S(1)} %fusion.at, f32[512,512]{1,0:T(8,128)S(1)} %copy-done.7, f32[256,512]{1,0:T(8,128)S(1)} %shard_map.166.second, f32[256,512]{1,0:T(8,128)S(1)} %shard_map.167.third, f32[64,128]{1,0:T(8,128)S(1)} %get-tuple-element.73.coarse, ...), custom_call_target="tpu_custom_call" | custom-call | flops 2684354560 | bytes 3735584 | tf_op jit(solution)/shard_map/pallas_call | solution.py:76
  85.2 1.6 shard_map.171
  86.9 2.8 %shard_map.172 = (bf16[128,1536]{1,0:T(8,128)(2,1)S(1)}, bf16[256,1536]{1,0:T(8,128)(2,1)S(1)}, bf16[128,1536]{1,0:T(8,128)(2,1)}) custom-call(s32[8]{0:T(128)S(1)} %fusion.at, bf16[1024,512]{1,0:T(8,128)(2,1)S(1)} %shard_map.168.refs_15_.grads, bf16[3072,256]{1,0:T(8,128)(2,1)S(1)} %bitcast.14, bf16[3072,128]{1,0:T(8,128)(2,1)S(1)} %bitcast.21, ...), custom_call_target="tpu_custom_call" | custom-call | flops 805306368 | bytes 5767200 | tf_op jit(solution)/shard_map/pallas_call | solution.py:76
  89.7 3.2 %collective-permute-start.15 = (bf16[256,768]{1,0:T(8,128)(2,1)S(1)}, bf16[256,768]{1,0:T(8,128)(2,1)S(1)}, u32[]{:S(2)}, u32[]{:S(2)}) collective-permute-start(bf16[256,768]{1,0:T(8,128)(2,1)S(1)} %get-tuple-element.46), channel_id=1, source_target_pairs={{0,3},{1,0},{2,1},{3,2},{4,7},{5,4},{6,5},{7,6},{8,11},{9,8},{10,9... | collective-permute-start | bytes 1179656 | tf_op jit(solution)/shard_map/ppermute | solution.py:60
  92.9 1.2 collective-permute-start.16
  94.1 0.8 collective-permute-start.23
  94.9 3.9 %shard_map.170 = (bf16[256,768]{1,0:T(8,128)(2,1)S(1)}, bf16[256,768]{1,0:T(8,128)(2,1)S(1)}, bf16[256,768]{1,0:T(8,128)(2,1)S(1)}, bf16[256,768]{1,0:T(8,128)(2...) custom-call(s32[8]{0:T(128)S(1)} %fusion.at, ...), custom_call_target="tpu_custom_call" | custom-call | flops 2013265920 | bytes 8126496 | tf_op jit(solution)/shard_map/pallas_call | solution.py:76
  99.5 2.1 %collective-permute-done.15.near_high = bf16[256,768]{1,0:T(8,128)(2,1)S(1)} collective-permute-done((bf16[256,768]{1,0:T(8,128)(2,1)S(1)}, bf16[256,768]{1,0:T(8,128)(2,1)S(1)}, u32[]{:S(2)}, u32[]{:S(2)}) %collective-permute-start.15) | collective-permute-done | bytes 393248 | tf_op jit(solution)/shard_map/ppermute | solution.py:60
  101.5 3.4 %collective-permute-done.16.arrived = bf16[128,1536]{1,0:T(8,128)(2,1)S(1)} collective-permute-done((bf16[128,1536]{1,0:T(8,128)(2,1)S(1)}, bf16[128,1536]{1,0:T(8,128)(2,1)S(1)}, u32[]{:S(2)}, u32[]{:S(2)}) %collective-permute-start.16) | collective-permute-done | bytes 393248 | tf_op jit(solution)/shard_map/ppermute | solution.py:52
  105.3 3.2 %collective-permute-start.20 = (bf16[384,768]{1,0:T(8,128)(2,1)S(1)}, bf16[384,768]{1,0:T(8,128)(2,1)S(1)}, u32[]{:S(2)}, u32[]{:S(2)}) collective-permute-start(bf16[384,768]{1,0:T(8,128)(2,1)S(1)} %get-tuple-element.52), channel_id=1, source_target_pairs={{0,3},{1,0},{2,1},{3,2},{4,7},{5,4},{6,5},{7,6},{8,11},{9,8},{10,9... | collective-permute-start | bytes 1769480 | tf_op jit(solution)/shard_map/ppermute | solution.py:60
  108.8 1.8 %collective-permute-start.19 = (bf16[256,768]{1,0:T(8,128)(2,1)S(1)}, bf16[256,768]{1,0:T(8,128)(2,1)S(1)}, u32[]{:S(2)}, u32[]{:S(2)}) collective-permute-start(bf16[256,768]{1,0:T(8,128)(2,1)S(1)} %get-tuple-element.51), channel_id=1, source_target_pairs={{0,1},{1,2},{2,3},{3,0},{4,5},{5,6},{6,7},{7,4},{8,9},{9,10},{10,1... | collective-permute-start | bytes 1179656 | tf_op jit(solution)/shard_map/ppermute | solution.py:56
  110.5 16.7 %collective-permute-done.18.above_low = bf16[256,768]{1,0:T(8,128)(2,1)S(1)} collective-permute-done((bf16[256,768]{1,0:T(8,128)(2,1)S(1)}, bf16[256,768]{1,0:T(8,128)(2,1)S(1)}, u32[]{:S(2)}, u32[]{:S(2)}) %collective-permute-start.18) | collective-permute-done | bytes 393248 | tf_op jit(solution)/shard_map/ppermute | solution.py:60
  127.2 1.7 %collective-permute-start.22 = (bf16[128,1536]{1,0:T(8,128)(2,1)}, bf16[128,1536]{1,0:T(8,128)(2,1)}, u32[]{:S(2)}, u32[]{:S(2)}) collective-permute-start(bf16[128,1536]{1,0:T(8,128)(2,1)} %get-tuple-element.56), channel_id=1, source_target_pairs={{0,4},{1,5},{2,6},{3,7},{4,0},{5,1},{6,2},{7,3},{8,12},{9,13},{10,... | collective-permute-start | bytes 1179656 | tf_op jit(solution)/shard_map/ppermute | solution.py:52
  128.9 1.1 shard_map.174
  130.0 0.7 collective-permute-start.21
  130.7 1.2 shard_map.175
  132.2 3.0 %collective-permute-start.25 = (bf16[128,1536]{1,0:T(8,128)(2,1)}, bf16[128,1536]{1,0:T(8,128)(2,1)}, u32[]{:S(2)}, u32[]{:S(2)}) collective-permute-start(bf16[128,1536]{1,0:T(8,128)(2,1)} %get-tuple-element.61), channel_id=1, source_target_pairs={{0,3},{1,0},{2,1},{3,2},{4,7},{5,4},{6,5},{7,6},{8,11},{9,8},{10,9... | collective-permute-start | bytes 1179656 | tf_op jit(solution)/shard_map/ppermute | solution.py:60
  135.2 8.7 %shard_map.169 = (bf16[3072,256]{1,0:T(8,128)(2,1)}, bf16[3072,128]{1,0:T(8,128)(2,1)}, bf16[3072,128]{1,0:T(8,128)(2,1)}, f32[1,3072]{1,0:T(1,128)S(1)}) custom-call(s32[8]{0:T(128)S(1)} %fusion.at, bf16[128,1792]{1,0:T(8,128)(2,1)} %get-tuple-element.37.refs_0_, bf16[128,1792]{1,0:T(8,128)(2,1)} %collective-permute-done.refs_1_, ...), custom_call_target="tpu_custom_call" | custom-call | flops 3221225472 | bytes 13643808 | tf_op jit(solution)/shard_map/pallas_call | solution.py:76
  143.9 1.8 %collective-permute-start.26 = (f32[1,3072]{1,0:T(1,128)S(1)}, f32[1,3072]{1,0:T(1,128)S(1)}, u32[]{:S(2)}, u32[]{:S(2)}) collective-permute-start(f32[1,3072]{1,0:T(1,128)S(1)} %get-tuple-element.62.mine), channel_id=1, source_target_pairs={{0,4},{1,5},{2,6},{3,7},{4,0},{5,1},{6,2},{7,3},{8,12},{9,13},{10,... | collective-permute-start | bytes 36872 | tf_op jit(solution)/shard_map/ppermute | solution.py:548
  145.7 2.0 %collective-permute-done.26.arrived = f32[1,3072]{1,0:T(1,128)S(1)} collective-permute-done((f32[1,3072]{1,0:T(1,128)S(1)}, f32[1,3072]{1,0:T(1,128)S(1)}, u32[]{:S(2)}, u32[]{:S(2)}) %collective-permute-start.26) | collective-permute-done | bytes 12320 | tf_op jit(solution)/shard_map/ppermute | solution.py:548
  147.7 3.7 %collective-permute-done.27.arrived = f32[1,3072]{1,0:T(1,128)S(1)} collective-permute-done((f32[1,3072]{1,0:T(1,128)S(1)}, f32[1,3072]{1,0:T(1,128)S(1)}, u32[]{:S(2)}, u32[]{:S(2)}) %collective-permute-start.27) | collective-permute-done | bytes 12320 | tf_op jit(solution)/shard_map/ppermute | solution.py:550
  151.3 1.5 collective-permute-start.28
  152.8 1.1 copy-done.8
  153.9 1.1 copy-done.9
  155.1 2.5 %shard_map.181 = (f32[64,3072]{1,0:T(8,128)}, f32[64,3072]{1,0:T(8,128)}) custom-call(f32[16,4,3072]{2,1,0:T(4,128)} %all-to-all-done.1.mean_parts, f32[64,3072]{1,0:T(8,128)S(1)} %copy-done.8, f32[64,3072]{1,0:T(8,128)S(1)} %copy-done.9), custom_call_target="tpu_custom_call" | custom-call | flops 100000 | bytes 3932160 | tf_op jit(solution)/shard_map/pallas_call | solution.py:76
  157.7 1.1 copy-done.5
  158.8 1.1 copy-done.11
  159.9 1.0 copy-done.14
  160.9 3.3 %shard_map.178 = (bf16[128,3072]{1,0:T(8,128)(2,1)}, f32[1,3072]{1,0:T(1,128)}) custom-call(bf16[128,3072]{1,0:T(8,128)(2,1)S(1)} %bitcast.32, f32[1,3072]{1,0:T(1,128)S(1)} %copy-done.16, f32[128,1536]{1,0:T(8,128)S(1)} %copy-done.11, bf16[128,1536]{1,0:T(8,128)(2,1)} %collective-permute-done.21.from_x, bf16[128,1536]{1,0:T(8,128)(2,1)S(1)} %copy-done.14, ...), custom_call_target="tpu_custom_call" | custom-call | flops 1000000 | bytes 4374528 | tf_op jit(solution)/shard_map/pallas_call | solution.py:76
  (71 shorter events, 4.1 us)
Async XLA Ops:
  0.6 1.1 copy-start.4
  1.8 0.7 copy-start.15
  3.9 23.4 %collective-permute-start = (bf16[128,1792]{1,0:T(8,128)(2,1)}, bf16[128,1792]{1,0:T(8,128)(2,1)}, u32[]{:S(2)}, u32[]{:S(2)}) collective-permute-start(bf16[128,1792]{1,0:T(8,128)(2,1)} %get-tuple-element.37.refs_0_), channel_id=1, source_target_pairs={{0,4},{1,5},{2,6},{3,7},{4,0},{5,1},{6,2},{7,3},{8,12},{9,13},{10,... | collective-permute-start | bytes 1376264 | tf_op jit(solution)/shard_map/ppermute | solution.py:52
  5.1 29.5 %collective-permute-start.1 = (bf16[128,1792]{1,0:T(8,128)(2,1)}, bf16[128,1792]{1,0:T(8,128)(2,1)}, u32[]{:S(2)}, u32[]{:S(2)}) collective-permute-start(bf16[128,1792]{1,0:T(8,128)(2,1)} %get-tuple-element.37.refs_0_), channel_id=1, source_target_pairs={{0,1},{1,2},{2,3},{3,0},{4,5},{5,6},{6,7},{7,4},{8,9},{9,10},{10,1... | collective-permute-start | bytes 1376264 | tf_op jit(solution)/shard_map/ppermute | solution.py:56
  6.7 26.6 %collective-permute-start.7 = (bf16[128,1280]{1,0:T(8,128)(2,1)}, bf16[128,1280]{1,0:T(8,128)(2,1)}, u32[]{:S(2)}, u32[]{:S(2)}) collective-permute-start(bf16[128,1280]{1,0:T(8,128)(2,1)} %get-tuple-element.38.refs_4_.refs_8_), channel_id=1, source_target_pairs={{0,4},{1,5},{2,6},{3,7},{4,0},{5,1},{6,2},{7,3},{8,12},{9,13},{10,... | collective-permute-start | bytes 983048 | tf_op jit(solution)/shard_map/ppermute | solution.py:52
  7.5 18.1 %collective-permute-start.8 = (bf16[128,1280]{1,0:T(8,128)(2,1)}, bf16[128,1280]{1,0:T(8,128)(2,1)S(1)}, u32[]{:S(2)}, u32[]{:S(2)}) collective-permute-start(bf16[128,1280]{1,0:T(8,128)(2,1)} %get-tuple-element.38.refs_4_.refs_8_), channel_id=1, source_target_pairs={{0,1},{1,2},{2,3},{3,0},{4,5},{5,6},{6,7},{7,4},{8,9},{9,10},{10,1... | collective-permute-start | bytes 983048 | tf_op jit(solution)/shard_map/ppermute | solution.py:56
  9.1 19.1 %collective-permute-start.9 = (bf16[128,1280]{1,0:T(8,128)(2,1)}, bf16[128,1280]{1,0:T(8,128)(2,1)}, u32[]{:S(2)}, u32[]{:S(2)}) collective-permute-start(bf16[128,1280]{1,0:T(8,128)(2,1)} %get-tuple-element.38.refs_4_.refs_8_), channel_id=1, source_target_pairs={{0,3},{1,0},{2,1},{3,2},{4,7},{5,4},{6,5},{7,6},{8,11},{9,8},{10,9... | collective-permute-start | bytes 983048 | tf_op jit(solution)/shard_map/ppermute | solution.py:60
  10.8 1.0 copy-start.12
  12.6 41.6 %copy-start.18 = (s32[8]{0:T(128)S(1)}, s32[8]{0:T(128)}, u32[]{:S(2)}) copy-start(s32[8]{0:T(128)} %constant.81.clone) | copy-start | bytes 100
  12.6 41.6 %copy-start.19 = (s32[8]{0:T(128)S(1)}, s32[8]{0:T(128)}, u32[]{:S(2)}) copy-start(s32[8]{0:T(128)} %constant.82.clone) | copy-start | bytes 100
  12.6 24.7 %all-to-all-start = ((bf16[16,4,3072]{2,1,0:T(4,128)(2,1)}), bf16[16,4,3072]{2,1,0:T(4,128)(2,1)}, u32[]{:S(2)}, u32[]{:S(2)}) async-start(bf16[16,4,3072]{2,1,0:T(4,128)(2,1)} %shard_map.179), calls=%async_computation | async-start | bytes 786432 | tf_op jit(solution)/shard_map/all_to_all | solution.py:569
  25.7 13.7 %collective-permute-start.2 = (bf16[128,1792]{1,0:T(8,128)(2,1)}, bf16[128,1792]{1,0:T(8,128)(2,1)}, u32[]{:S(2)}, u32[]{:S(2)}) collective-permute-start(bf16[128,1792]{1,0:T(8,128)(2,1)} %get-tuple-element.37.refs_0_), channel_id=1, source_target_pairs={{0,3},{1,0},{2,1},{3,2},{4,7},{5,4},{6,5},{7,6},{8,11},{9,8},{10,9... | collective-permute-start | bytes 1376264 | tf_op jit(solution)/shard_map/ppermute | solution.py:60
  27.4 23.7 %collective-permute-start.4 = (bf16[128,1792]{1,0:T(8,128)(2,1)}, bf16[128,1792]{1,0:T(8,128)(2,1)}, u32[]{:S(2)}, u32[]{:S(2)}) collective-permute-start(bf16[128,1792]{1,0:T(8,128)(2,1)} %collective-permute-done.refs_1_), channel_id=1, source_target_pairs={{0,3},{1,0},{2,1},{3,2},{4,7},{5,4},{6,5},{7,6},{8,11},{9,8},{10,9... | collective-permute-start | bytes 1376264 | tf_op jit(solution)/shard_map/ppermute | solution.py:60
  28.2 29.8 %copy-start = (bf16[1,3072,256]{2,1,0:T(8,128)(2,1)S(1)}, bf16[1,3072,256]{2,1,0:T(8,128)(2,1)}, u32[]{:S(2)}) copy-start(bf16[1,3072,256]{2,1,0:T(8,128)(2,1)} %param.13) | copy-start | bytes 4718596
  28.2 29.8 %copy-start.1 = (bf16[1,3072,128]{2,1,0:T(8,128)(2,1)S(1)}, bf16[1,3072,128]{2,1,0:T(8,128)(2,1)}, u32[]{:S(2)}) copy-start(bf16[1,3072,128]{2,1,0:T(8,128)(2,1)} %param.14) | copy-start | bytes 2359300
  28.2 29.8 %copy-start.2 = (bf16[1,3072,128]{2,1,0:T(8,128)(2,1)S(1)}, bf16[1,3072,128]{2,1,0:T(8,128)(2,1)}, u32[]{:S(2)}) copy-start(bf16[1,3072,128]{2,1,0:T(8,128)(2,1)} %param.15) | copy-start | bytes 2359300
  30.2 41.9 %collective-permute-start.10 = (bf16[256,1280]{1,0:T(8,128)(2,1)}, bf16[256,1280]{1,0:T(8,128)(2,1)}, u32[]{:S(2)}, u32[]{:S(2)}) collective-permute-start(bf16[256,1280]{1,0:T(8,128)(2,1)} %shard_map.163), channel_id=1, source_target_pairs={{0,4},{1,5},{2,6},{3,7},{4,0},{5,1},{6,2},{7,3},{8,12},{9,13},{10,... | collective-permute-start | bytes 1966088 | tf_op jit(solution)/shard_map/ppermute | solution.py:52
  33.3 6.8 %collective-permute-start.11 = (bf16[64,1280]{1,0:T(8,128)(2,1)}, bf16[64,1280]{1,0:T(8,128)(2,1)}, u32[]{:S(2)}, u32[]{:S(2)}) collective-permute-start(bf16[64,1280]{1,0:T(8,128)(2,1)} %slice.8), channel_id=1, source_target_pairs={{0,1},{1,2},{2,3},{3,0},{4,5},{5,6},{6,7},{7,4},{8,9},{9,10},{10,1... | collective-permute-start | bytes 491528 | tf_op jit(solution)/shard_map/ppermute | solution.py:56
  34.6 15.9 %collective-permute-start.12 = (bf16[64,1280]{1,0:T(8,128)(2,1)}, bf16[64,1280]{1,0:T(8,128)(2,1)}, u32[]{:S(2)}, u32[]{:S(2)}) collective-permute-start(bf16[64,1280]{1,0:T(8,128)(2,1)} %slice.9), channel_id=1, source_target_pairs={{0,3},{1,0},{2,1},{3,2},{4,7},{5,4},{6,5},{7,6},{8,11},{9,8},{10,9... | collective-permute-start | bytes 491528 | tf_op jit(solution)/shard_map/ppermute | solution.py:60
  39.4 32.7 %collective-permute-start.3 = (bf16[128,1792]{1,0:T(8,128)(2,1)}, bf16[128,1792]{1,0:T(8,128)(2,1)}, u32[]{:S(2)}, u32[]{:S(2)}) collective-permute-start(bf16[128,1792]{1,0:T(8,128)(2,1)} %collective-permute-done.refs_1_), channel_id=1, source_target_pairs={{0,1},{1,2},{2,3},{3,0},{4,5},{5,6},{6,7},{7,4},{8,9},{9,10},{10,1... | collective-permute-start | bytes 1376264 | tf_op jit(solution)/shard_map/ppermute | solution.py:56
  40.2 34.3 %collective-permute-start.5 = (bf16[128,1792]{1,0:T(8,128)(2,1)}, bf16[128,1792]{1,0:T(8,128)(2,1)}, u32[]{:S(2)}, u32[]{:S(2)}) collective-permute-start(bf16[128,1792]{1,0:T(8,128)(2,1)} %collective-permute-done.1.refs_2_), channel_id=1, source_target_pairs={{0,1},{1,2},{2,3},{3,0},{4,5},{5,6},{6,7},{7,4},{8,9},{9,10},{10,1... | collective-permute-start | bytes 1376264 | tf_op jit(solution)/shard_map/ppermute | solution.py:56
  50.5 5.6 %collective-permute-start.29 = (f32[4,3072]{1,0:T(4,128)S(1)}, f32[4,3072]{1,0:T(4,128)S(1)}, u32[]{:S(2)}, u32[]{:S(2)}) collective-permute-start(f32[4,3072]{1,0:T(4,128)S(1)} %subtract_reduce_fusion.mine), channel_id=1, source_target_pairs={{0,128},{8,136},{16,144},{24,152},{32,160},{40,168},{48,176},{56,1... | collective-permute-start | bytes 147464 | tf_op jit(solution)/shard_map/ppermute | solution.py:575
  51.1 23.4 %collective-permute-start.6 = (bf16[128,1792]{1,0:T(8,128)(2,1)}, bf16[128,1792]{1,0:T(8,128)(2,1)}, u32[]{:S(2)}, u32[]{:S(2)}) collective-permute-start(bf16[128,1792]{1,0:T(8,128)(2,1)} %collective-permute-done.4.refs_1_.refs_5_), channel_id=1, source_target_pairs={{0,3},{1,0},{2,1},{3,2},{4,7},{5,4},{6,5},{7,6},{8,11},{9,8},{10,9... | collective-permute-start | bytes 1376264 | tf_op jit(solution)/shard_map/ppermute | solution.py:60
  56.1 18.3 %collective-permute-start.13 = (bf16[128,1280]{1,0:T(8,128)(2,1)}, bf16[128,1280]{1,0:T(8,128)(2,1)}, u32[]{:S(2)}, u32[]{:S(2)}) collective-permute-start(bf16[128,1280]{1,0:T(8,128)(2,1)} %shard_map.164.refs_2_.refs_13_), channel_id=1, source_target_pairs={{0,4},{1,5},{2,6},{3,7},{4,0},{5,1},{6,2},{7,3},{8,12},{9,13},{10,... | collective-permute-start | bytes 983048 | tf_op jit(solution)/shard_map/ppermute | solution.py:52
  61.5 1.0 copy-start.6
  62.6 0.9 copy-start.3
  63.5 89.4 %all-to-all-start.1 = ((f32[16,4,3072]{2,1,0:T(4,128)}), f32[16,4,3072]{2,1,0:T(4,128)}, u32[]{:S(2)}, u32[]{:S(2)}) async-start(f32[16,4,3072]{2,1,0:T(4,128)} %copy-done.3), calls=%async_computation.1 | async-start | bytes 1572864 | tf_op jit(solution)/shard_map/all_to_all | solution.py:579
  74.4 2.5 %copy-start.7 = (f32[512,512]{1,0:T(8,128)S(1)}, f32[512,512]{1,0:T(8,128)}, u32[]{:S(2)}) copy-start(f32[512,512]{1,0:T(8,128)} %copy-done.6) | copy-start | bytes 3145732
  74.5 2.5 %copy-start.17 = (bf16[1,1024,256]{2,1,0:T(8,128)(2,1)S(1)}, bf16[1,1024,256]{2,1,0:T(8,128)(2,1)}, u32[]{:S(2)}) copy-start(bf16[1,1024,256]{2,1,0:T(8,128)(2,1)} %param.16) | copy-start | bytes 1572868
  86.8 12.7 %collective-permute-start.14 = (bf16[256,768]{1,0:T(8,128)(2,1)S(1)}, bf16[256,768]{1,0:T(8,128)(2,1)S(1)}, u32[]{:S(2)}, u32[]{:S(2)}) collective-permute-start(bf16[256,768]{1,0:T(8,128)(2,1)S(1)} %get-tuple-element.44), channel_id=1, source_target_pairs={{0,1},{1,2},{2,3},{3,0},{4,5},{5,6},{6,7},{7,4},{8,9},{9,10},{10,1... | collective-permute-start | bytes 1179656 | tf_op jit(solution)/shard_map/ppermute | solution.py:56
  89.7 11.8 %collective-permute-start.15 = (bf16[256,768]{1,0:T(8,128)(2,1)S(1)}, bf16[256,768]{1,0:T(8,128)(2,1)S(1)}, u32[]{:S(2)}, u32[]{:S(2)}) collective-permute-start(bf16[256,768]{1,0:T(8,128)(2,1)S(1)} %get-tuple-element.46), channel_id=1, source_target_pairs={{0,3},{1,0},{2,1},{3,2},{4,7},{5,4},{6,5},{7,6},{8,11},{9,8},{10,9... | collective-permute-start | bytes 1179656 | tf_op jit(solution)/shard_map/ppermute | solution.py:60
  92.9 12.0 %collective-permute-start.16 = (bf16[128,1536]{1,0:T(8,128)(2,1)S(1)}, bf16[128,1536]{1,0:T(8,128)(2,1)S(1)}, u32[]{:S(2)}, u32[]{:S(2)}) collective-permute-start(bf16[128,1536]{1,0:T(8,128)(2,1)S(1)} %get-tuple-element.48), channel_id=1, source_target_pairs={{0,4},{1,5},{2,6},{3,7},{4,0},{5,1},{6,2},{7,3},{8,12},{9,13},{10,... | collective-permute-start | bytes 1179656 | tf_op jit(solution)/shard_map/ppermute | solution.py:52
  94.1 36.6 %collective-permute-start.23 = (bf16[256,1536]{1,0:T(8,128)(2,1)S(1)}, bf16[256,1536]{1,0:T(8,128)(2,1)S(1)}, u32[]{:S(2)}, u32[]{:S(2)}) collective-permute-start(bf16[256,1536]{1,0:T(8,128)(2,1)S(1)} %get-tuple-element.59), channel_id=1, source_target_pairs={{0,4},{1,5},{2,6},{3,7},{4,0},{5,1},{6,2},{7,3},{8,12},{9,13},{10,... | collective-permute-start | bytes 2359304 | tf_op jit(solution)/shard_map/ppermute | solution.py:52
  98.8 30.1 %copy-start.13 = (bf16[128,1536]{1,0:T(8,128)(2,1)}, bf16[128,1536]{1,0:T(8,128)(2,1)S(1)}, u32[]{:S(2)}) copy-start(bf16[128,1536]{1,0:T(8,128)(2,1)S(1)} %get-tuple-element.55.q0) | copy-start | bytes 1179652
  105.2 23.7 %collective-permute-start.17 = (bf16[384,768]{1,0:T(8,128)(2,1)S(1)}, bf16[384,768]{1,0:T(8,128)(2,1)S(1)}, u32[]{:S(2)}, u32[]{:S(2)}) collective-permute-start(bf16[384,768]{1,0:T(8,128)(2,1)S(1)} %get-tuple-element.49), channel_id=1, source_target_pairs={{0,1},{1,2},{2,3},{3,0},{4,5},{5,6},{6,7},{7,4},{8,9},{9,10},{10,1... | collective-permute-start | bytes 1769480 | tf_op jit(solution)/shard_map/ppermute | solution.py:56
  105.3 23.7 %collective-permute-start.20 = (bf16[384,768]{1,0:T(8,128)(2,1)S(1)}, bf16[384,768]{1,0:T(8,128)(2,1)S(1)}, u32[]{:S(2)}, u32[]{:S(2)}) collective-permute-start(bf16[384,768]{1,0:T(8,128)(2,1)S(1)} %get-tuple-element.52), channel_id=1, source_target_pairs={{0,3},{1,0},{2,1},{3,2},{4,7},{5,4},{6,5},{7,6},{8,11},{9,8},{10,9... | collective-permute-start | bytes 1769480 | tf_op jit(solution)/shard_map/ppermute | solution.py:60
  108.5 18.7 %collective-permute-start.18 = (bf16[256,768]{1,0:T(8,128)(2,1)S(1)}, bf16[256,768]{1,0:T(8,128)(2,1)S(1)}, u32[]{:S(2)}, u32[]{:S(2)}) collective-permute-start(bf16[256,768]{1,0:T(8,128)(2,1)S(1)} %get-tuple-element.50), channel_id=1, source_target_pairs={{0,3},{1,0},{2,1},{3,2},{4,7},{5,4},{6,5},{7,6},{8,11},{9,8},{10,9... | collective-permute-start | bytes 1179656 | tf_op jit(solution)/shard_map/ppermute | solution.py:60
  108.8 20.2 %collective-permute-start.19 = (bf16[256,768]{1,0:T(8,128)(2,1)S(1)}, bf16[256,768]{1,0:T(8,128)(2,1)S(1)}, u32[]{:S(2)}, u32[]{:S(2)}) collective-permute-start(bf16[256,768]{1,0:T(8,128)(2,1)S(1)} %get-tuple-element.51), channel_id=1, source_target_pairs={{0,1},{1,2},{2,3},{3,0},{4,5},{5,6},{6,7},{7,4},{8,9},{9,10},{10,1... | collective-permute-start | bytes 1179656 | tf_op jit(solution)/shard_map/ppermute | solution.py:56
  127.2 30.4 %collective-permute-start.22 = (bf16[128,1536]{1,0:T(8,128)(2,1)}, bf16[128,1536]{1,0:T(8,128)(2,1)}, u32[]{:S(2)}, u32[]{:S(2)}) collective-permute-start(bf16[128,1536]{1,0:T(8,128)(2,1)} %get-tuple-element.56), channel_id=1, source_target_pairs={{0,4},{1,5},{2,6},{3,7},{4,0},{5,1},{6,2},{7,3},{8,12},{9,13},{10,... | collective-permute-start | bytes 1179656 | tf_op jit(solution)/shard_map/ppermute | solution.py:52
  130.0 1.9 %copy-start.10 = (f32[128,1536]{1,0:T(8,128)}, f32[128,1536]{1,0:T(8,128)S(1)}, u32[]{:S(2)}) copy-start(f32[128,1536]{1,0:T(8,128)S(1)} %get-tuple-element.53.own_a) | copy-start | bytes 2359300
  130.0 27.6 %collective-permute-start.21 = (bf16[128,1536]{1,0:T(8,128)(2,1)}, bf16[128,1536]{1,0:T(8,128)(2,1)}, u32[]{:S(2)}, u32[]{:S(2)}) collective-permute-start(bf16[128,1536]{1,0:T(8,128)(2,1)} %get-tuple-element.54), channel_id=1, source_target_pairs={{0,4},{1,5},{2,6},{3,7},{4,0},{5,1},{6,2},{7,3},{8,12},{9,13},{10,... | collective-permute-start | bytes 1179656 | tf_op jit(solution)/shard_map/ppermute | solution.py:52
  131.9 25.7 %collective-permute-start.24 = (bf16[128,1536]{1,0:T(8,128)(2,1)}, bf16[128,1536]{1,0:T(8,128)(2,1)}, u32[]{:S(2)}, u32[]{:S(2)}) collective-permute-start(bf16[128,1536]{1,0:T(8,128)(2,1)} %get-tuple-element.60), channel_id=1, source_target_pairs={{0,1},{1,2},{2,3},{3,0},{4,5},{5,6},{6,7},{7,4},{8,9},{9,10},{10,1... | collective-permute-start | bytes 1179656 | tf_op jit(solution)/shard_map/ppermute | solution.py:56
  132.2 25.4 %collective-permute-start.25 = (bf16[128,1536]{1,0:T(8,128)(2,1)}, bf16[128,1536]{1,0:T(8,128)(2,1)}, u32[]{:S(2)}, u32[]{:S(2)}) collective-permute-start(bf16[128,1536]{1,0:T(8,128)(2,1)} %get-tuple-element.61), channel_id=1, source_target_pairs={{0,3},{1,0},{2,1},{3,2},{4,7},{5,4},{6,5},{7,6},{8,11},{9,8},{10,9... | collective-permute-start | bytes 1179656 | tf_op jit(solution)/shard_map/ppermute | solution.py:60
  143.9 13.7 %copy-start.16 = (f32[1,3072]{1,0:T(1,128)S(1)}, f32[1,3072]{1,0:T(1,128)}, u32[]{:S(2)}) copy-start(f32[1,3072]{1,0:T(1,128)} %gain.3) | copy-start | bytes 36868
  143.9 3.7 %collective-permute-start.26 = (f32[1,3072]{1,0:T(1,128)S(1)}, f32[1,3072]{1,0:T(1,128)S(1)}, u32[]{:S(2)}, u32[]{:S(2)}) collective-permute-start(f32[1,3072]{1,0:T(1,128)S(1)} %get-tuple-element.62.mine), channel_id=1, source_target_pairs={{0,4},{1,5},{2,6},{3,7},{4,0},{5,1},{6,2},{7,3},{8,12},{9,13},{10,... | collective-permute-start | bytes 36872 | tf_op jit(solution)/shard_map/ppermute | solution.py:548
  147.6 3.7 %collective-permute-start.27 = (f32[1,3072]{1,0:T(1,128)S(1)}, f32[1,3072]{1,0:T(1,128)S(1)}, u32[]{:S(2)}, u32[]{:S(2)}) collective-permute-start(f32[1,3072]{1,0:T(1,128)S(1)} %shard_map.176.mine), channel_id=1, source_target_pairs={{0,1},{1,0},{2,3},{3,2},{4,5},{5,4},{6,7},{7,6},{8,9},{9,8},{10,11... | collective-permute-start | bytes 36872 | tf_op jit(solution)/shard_map/ppermute | solution.py:550
  151.3 6.3 %collective-permute-start.28 = (f32[1,3072]{1,0:T(1,128)S(1)}, f32[1,3072]{1,0:T(1,128)S(1)}, u32[]{:S(2)}, u32[]{:S(2)}) collective-permute-start(f32[1,3072]{1,0:T(1,128)S(1)} %shard_map.177.part), channel_id=1, source_target_pairs={{0,2},{1,3},{2,0},{3,1},{4,6},{5,7},{6,4},{7,5},{8,10},{9,11},{10,... | collective-permute-start | bytes 36872 | tf_op jit(solution)/shard_map/ppermute | solution.py:552
  152.8 1.1 copy-start.8
  153.9 1.1 copy-start.9
  157.6 1.1 copy-start.5
  158.8 1.1 copy-start.11
  159.9 1.0 copy-start.14
